TPU v7x, 128 devices: a whole 4x4x4 slice. The times are simulated.
128 devices in a mesh: tp: 16 (over x_lo, z, core), seq: 8 (over y, x_hi).
Axes of the slice: x: 4 (x_hi: 2, x_lo: 2; x = x_hi * 2 + x_lo), y: 4, z: 4, core: 2. Of those that a mesh axis runs over, the one named last changes fastest.
Arguments:
- residual: bfloat16 [2048, 4096], P('seq'), may hold values from -6 to 6
- mix_gain: float32 [4096], replicated, may hold values from 0.5 to 1.5
- in_proj: bfloat16 [4096, 4096], P(None, 'tp'), may hold values from -0.09375 to 0.09375
- branch_proj: bfloat16 [4096, 4096], P(None, 'tp'), may hold values from -0.09375 to 0.09375
- conv_weight: float32 [4, 4096], P(None, 'tp'), may hold values from -3 to 3
- conv_bias: float32 [4096], P('tp'), may hold values from -1.25 to 1.25
- input_gate: bfloat16 [16, 256, 256], P('tp'), may hold values from -0.375 to 0.375
- input_bias: float32 [4096], P('tp'), may hold values from -3 to 3
- decay_gate: bfloat16 [16, 256, 256], P('tp'), may hold values from -0.375 to 0.375
- decay_bias: float32 [4096], P('tp'), may hold values from -3 to 3
- decay_param: float32 [4096], P('tp'), may hold values from -13 to -2, as said below
- out_proj: bfloat16 [4096, 4096], P('tp'), may hold values from -0.25 to 0.25
- mlp_gain: float32 [4096], replicated, may hold values from 0.5 to 1.5
- gate_proj: bfloat16 [4096, 12288], P('seq', 'tp'), may hold values from -0.09375 to 0.09375
- up_proj: bfloat16 [4096, 12288], P('seq', 'tp'), may hold values from -0.09375 to 0.09375
- down_proj: bfloat16 [12288, 4096], P('tp'), may hold values from -0.078125 to 0.078125
Outputs:
- updated: bfloat16 [2048, 4096], P('seq')
Inputs may be any that keep to these rules, and one draw needn't show every extreme that they name: softplus(decay_param) lies between 0.02 / 2048 and 0.1 for every channel.
All inputs are finite; a program needn't handle non-finite values.
Results may differ from a plain program's by a relative error of at most 0.02.
Values may be sent and summed in bfloat16 or wider, within the bound.
A program may use at most 128 MiB of HBM per device.

v0:
```python
import functools

import jax
import jax.numpy as jnp
from jax import lax
from jax.experimental import pallas as pl
from jax.experimental.pallas import tpu as pltpu
from jax.sharding import PartitionSpec as P

epsilon = 1e-06
LOGICAL = pl.DeviceIdType.MESH
LANES = 128
EDGE = 16
HEIGHT = 16
LAG = 4


def greet(axis, peers):
    barrier = pltpu.get_barrier_semaphore()
    for peer in peers:
        pl.semaphore_signal(barrier, inc=1, device_id={axis: peer}, device_id_type=LOGICAL)
    pl.semaphore_wait(barrier, len(peers))


def one_minus_exp(x):
    series = 1.0 + x * (1.0 / 9.0)
    for k in range(8, 1, -1):
        series = 1.0 + x * (1.0 / k) * series
    return jnp.where(x > -0.5, -x * series, 1.0 - jnp.exp(x))


def recurrence_kernel(
    count,
    taps,
    inner_ref,
    branch_ref,
    conv_weight_ref,
    conv_bias_ref,
    input_gate_ref,
    input_bias_ref,
    decay_gate_ref,
    decay_bias_ref,
    slope_ref,
    gated_ref,
    tail_ref,
    decays_ref,
    states_ref,
    ends_ref,
    arrived_ref,
    tail_send,
    tail_recv,
    end_send,
    end_recv,
):
    me = lax.axis_index("seq")
    length, channels = inner_ref.shape
    heads, head = input_gate_ref.shape[0], input_gate_ref.shape[1]
    peers = [lax.rem(me + offset, count) for offset in range(1, count)]
    greet("seq", peers)
    tail_copy = pltpu.make_async_remote_copy(
        src_ref=inner_ref.at[pl.ds(length - EDGE, EDGE), :],
        dst_ref=tail_ref,
        send_sem=tail_send,
        recv_sem=tail_recv,
        device_id={"seq": lax.rem(me + 1, count)},
        device_id_type=LOGICAL,
    )
    tail_copy.start()
    tail_copy.wait()
    follows = jnp.where(me > 0, 1.0, 0.0)

    for h in range(heads):
        columns = pl.ds(h * head, head)
        row = lax.broadcasted_iota(jnp.int32, (length, head), 0)
        current = inner_ref[:, columns].astype(jnp.float32)
        tail = tail_ref[:, columns].astype(jnp.float32) * follows
        before = jnp.concatenate([tail, jnp.zeros((length - EDGE, head), jnp.float32)], axis=0)
        total = conv_bias_ref[:, columns] + conv_weight_ref[0:1, columns] * current
        for tap in range(1, taps):
            shifted = jnp.where(
                row < tap,
                pltpu.roll(before, length + tap - EDGE, 0),
                pltpu.roll(current, tap, 0),
            )
            total = total + conv_weight_ref[tap : tap + 1, columns] * shifted
        smoothed = total.astype(jnp.bfloat16)
        input_rate = jax.nn.sigmoid(
            jnp.dot(smoothed, input_gate_ref[h], preferred_element_type=jnp.float32)
            + input_bias_ref[:, columns]
        )
        decay_rate = jax.nn.sigmoid(
            jnp.dot(smoothed, decay_gate_ref[h], preferred_element_type=jnp.float32)
            + decay_bias_ref[:, columns]
        )
        log_decay = decay_rate * slope_ref[:, columns]
        scale_in = jnp.sqrt(one_minus_exp(2.0 * log_decay))
        scale_in = jnp.where(jnp.logical_and(row == 0, me == 0), 1.0, scale_in)
        decays_ref[:, columns] = jnp.exp(log_decay)
        states_ref[:, columns] = smoothed.astype(jnp.float32) * input_rate * scale_in

    for c in range(channels // LANES):
        columns = pl.ds(c * LANES, LANES)
        row = lax.broadcasted_iota(jnp.int32, (length, LANES), 0)
        decay, state = decays_ref[:, columns], states_ref[:, columns]
        step = 1
        while step < length:
            reached = row >= step
            state = state + decay * jnp.where(reached, pltpu.roll(state, step, 0), 0.0)
            decay = decay * jnp.where(reached, pltpu.roll(decay, step, 0), 1.0)
            step *= 2
        decays_ref[:, columns] = decay
        states_ref[:, columns] = state
        ends_ref[0:1, columns] = decay[length - 1 :, :]
        ends_ref[1:2, columns] = state[length - 1 :, :]

    copies = [
        pltpu.make_async_remote_copy(
            src_ref=ends_ref,
            dst_ref=arrived_ref.at[k],
            send_sem=end_send.at[k],
            recv_sem=end_recv.at[k],
            device_id={"seq": peers[k]},
            device_id_type=LOGICAL,
        )
        for k in range(count - 1)
    ]
    for copy in copies:
        copy.start()
    for copy in copies:
        copy.wait()
    carried = jnp.zeros((1, channels), jnp.float32)
    for k in range(count - 2, -1, -1):
        new = arrived_ref[k, 0:1, :] * carried + arrived_ref[k, 1:2, :]
        carried = jnp.where(me >= k + 1, new, carried)
    gated_ref[...] = (
        (states_ref[...] + decays_ref[...] * carried) * branch_ref[...]
    ).astype(jnp.bfloat16)


def recurrence(inner, branch, conv_weight, conv_bias, input_gate, input_bias, decay_gate, decay_bias, slope):
    count = lax.axis_size("seq")
    length, channels = inner.shape
    vmem = pl.BlockSpec(memory_space=pltpu.VMEM)
    return pl.pallas_call(
        functools.partial(recurrence_kernel, count, conv_weight.shape[0]),
        out_shape=jax.ShapeDtypeStruct((length, channels), jnp.bfloat16),
        in_specs=[vmem] * 9,
        out_specs=vmem,
        scratch_shapes=[
            pltpu.VMEM((EDGE, channels), jnp.bfloat16),
            pltpu.VMEM((length, channels), jnp.float32),
            pltpu.VMEM((length, channels), jnp.float32),
            pltpu.VMEM((8, channels), jnp.float32),
            pltpu.VMEM((count - 1, 8, channels), jnp.float32),
            pltpu.SemaphoreType.DMA,
            pltpu.SemaphoreType.DMA,
            pltpu.SemaphoreType.DMA((count - 1,)),
            pltpu.SemaphoreType.DMA((count - 1,)),
        ],
        compiler_params=pltpu.CompilerParams(
            collective_id=0, has_side_effects=True, vmem_limit_bytes=24 * 2**20
        ),
    )(
        inner,
        branch,
        conv_weight,
        conv_bias[None],
        input_gate,
        input_bias[None],
        decay_gate,
        decay_bias[None],
        slope[None],
    )


def summed_rows(product, extent, axis):
    everything = product(jnp.int32(0), lax.axis_size(axis) * extent)
    own = lax.psum_scatter(everything.astype(jnp.bfloat16), axis, scatter_dimension=0, tiled=True)
    return own.astype(jnp.float32)


def rms_norm(values, gain):
    wide = values.astype(jnp.float32)
    factor = lax.rsqrt(jnp.mean(wide * wide, axis=-1, keepdims=True) + epsilon)
    return (wide * factor * gain).astype(jnp.bfloat16)


def summed_kernel(
    chips,
    part_ref,
    base_ref,
    out_ref,
    pair_ref,
    stage_ref,
    left_ref,
    right_ref,
    pair_send,
    pair_recv,
    line_send,
    left_recv,
    right_recv,
    out_send,
    out_recv,
    share_send,
    share_recv,
):
    me = lax.axis_index("tp")
    core, chip = lax.rem(me, 2), lax.div(me, 2)
    partner = me + 1 - 2 * core
    pieces, height = stage_ref.shape[0], stage_ref.shape[1]
    half = pieces * height
    ring = [partner, lax.rem(me + 2, 2 * chips), lax.rem(me + 2 * chips - 2, 2 * chips)]
    greet("tp", ring)

    def rows(which, p):
        return pl.ds(pl.multiple_of(which * half + p * height, height), height)

    def remote(source, target, send, recv, device):
        return pltpu.make_async_remote_copy(
            src_ref=source,
            dst_ref=target,
            send_sem=send,
            recv_sem=recv,
            device_id={"tp": device},
            device_id_type=LOGICAL,
        )

    def pair(p):
        return remote(
            part_ref.at[rows(1 - core, p), :], pair_ref.at[p], pair_send.at[p], pair_recv.at[p], partner
        )

    def rightward(p):
        return remote(stage_ref.at[p], left_ref.at[p], line_send.at[p], left_recv.at[p], me + 2)

    def leftward(p):
        return remote(stage_ref.at[p], right_ref.at[p], line_send.at[p], right_recv.at[p], me - 2)

    def outward(p, way):
        mine = out_ref.at[rows(core, p), :]
        return remote(mine, mine, out_send.at[way, p], out_recv.at[p], me + 4 * way - 2)

    def share(p, which):
        block = out_ref.at[rows(which, p), :]
        return remote(block, block, share_send.at[p], share_recv.at[p], partner)

    for p in range(pieces):
        pair(p).start()

    def run(z):
        sent = []

        def owner(p):
            return chips // 2 - p % 2

        def start(copy):
            copy.start()
            sent.append(copy)

        def reduce(p):
            pair(p).wait_recv()
            value = part_ref[rows(core, p), :].astype(jnp.float32) + pair_ref[p].astype(jnp.float32)
            if z > 0 and z <= owner(p):
                rightward(p).wait_recv()
                value = value + left_ref[p].astype(jnp.float32)
            if z < chips - 1 and z >= owner(p):
                leftward(p).wait_recv()
                value = value + right_ref[p].astype(jnp.float32)
            if z == owner(p):
                total = value + base_ref[rows(core, p), :].astype(jnp.float32)
                out_ref[rows(core, p), :] = total.astype(out_ref.dtype)
                if z > 0:
                    start(outward(p, 0))
                if z < chips - 1:
                    start(outward(p, 1))
                start(share(p, core))
            else:
                stage_ref[p] = value.astype(stage_ref.dtype)
                start(rightward(p) if z < owner(p) else leftward(p))

        def spread(p):
            if z == owner(p):
                return
            outward(p, 0).wait_recv()
            if z < owner(p) and z > 0:
                start(outward(p, 0))
            if z > owner(p) and z < chips - 1:
                start(outward(p, 1))
            start(share(p, core))

        lag = pieces if z in (0, chips - 1) else min(pieces, LAG)
        for p in range(pieces + lag):
            if p < pieces:
                reduce(p)
            if p >= lag:
                spread(p - lag)
        for copy in sent:
            copy.wait_send()

    for z in range(chips):
        pl.when(chip == z)(functools.partial(run, z))
    for p in range(pieces):
        pair(p).wait_send()
        share(p, 1 - core).wait_recv()


def summed(part, base, call):
    chips = lax.axis_size("tp") // 2
    length, width = part.shape
    pieces = length // (2 * HEIGHT)
    vmem = pl.BlockSpec(memory_space=pltpu.VMEM)
    block = pltpu.VMEM((pieces, HEIGHT, width), jnp.bfloat16)
    semaphores = pltpu.SemaphoreType.DMA((pieces,))
    return pl.pallas_call(
        functools.partial(summed_kernel, chips),
        out_shape=jax.ShapeDtypeStruct((length, width), jnp.bfloat16),
        in_specs=[vmem] * 2,
        out_specs=vmem,
        scratch_shapes=[block] * 4
        + [semaphores] * 5
        + [pltpu.SemaphoreType.DMA((2, pieces))]
        + [semaphores] * 3,
        compiler_params=pltpu.CompilerParams(
            collective_id=call, has_side_effects=True, vmem_limit_bytes=24 * 2**20
        ),
    )(part, base)


def on_device(
    residual,
    mix_gain,
    in_proj,
    branch_proj,
    conv_weight,
    conv_bias,
    input_gate,
    input_bias,
    decay_gate,
    decay_bias,
    decay_param,
    out_proj,
    mlp_gain,
    gate_proj,
    up_proj,
    down_proj,
):
    length = residual.shape[0]
    normed = rms_norm(residual, mix_gain)
    branch = jax.nn.gelu(
        jnp.dot(normed, branch_proj, preferred_element_type=jnp.float32), approximate=True
    )
    inner = jnp.dot(normed, in_proj, preferred_element_type=jnp.float32).astype(jnp.bfloat16)
    gated = recurrence(
        inner,
        branch,
        conv_weight,
        conv_bias,
        input_gate,
        input_bias,
        decay_gate,
        decay_bias,
        -8.0 * jax.nn.softplus(decay_param),
    )
    mixed = jnp.dot(gated, out_proj, preferred_element_type=jnp.float32).astype(jnp.bfloat16)
    middle = summed(mixed, residual, 1)
    hidden_in = rms_norm(middle, mlp_gain)
    width = gate_proj.shape[1]
    columns = lax.all_to_all(hidden_in, "seq", split_axis=1, concat_axis=0, tiled=True)

    def term(start, count):
        block = lax.dynamic_slice_in_dim(columns, start, count, 0)
        return jnp.concatenate(
            [
                jnp.dot(block, gate_proj, preferred_element_type=jnp.float32),
                jnp.dot(block, up_proj, preferred_element_type=jnp.float32),
            ],
            axis=1,
        )

    joined = summed_rows(term, length, "seq")
    gate = joined[:, :width]
    up = joined[:, width:]
    hidden = (jax.nn.gelu(gate, approximate=True) * up).astype(jnp.bfloat16)
    output = jnp.dot(hidden, down_proj, preferred_element_type=jnp.float32).astype(jnp.bfloat16)
    return summed(output, middle, 2)


def solution(mesh):
    in_specs = (
        P("seq", None),
        P(),
        P(None, "tp"),
        P(None, "tp"),
        P(None, "tp"),
        P("tp"),
        P("tp", None, None),
        P("tp"),
        P("tp", None, None),
        P("tp"),
        P("tp"),
        P("tp", None),
        P(),
        P("seq", "tp"),
        P("seq", "tp"),
        P("tp", None),
    )
    out_specs = P("seq", None)
    return jax.shard_map(
        on_device, mesh=mesh, in_specs=in_specs, out_specs=out_specs, check_vma=False
    )
```

profile of v0, /device:TPU:1, one launch (start us, length us, event | category | flops | bytes accessed | tf_op | source)
XLA Modules:
  0.0 396.0 jit_solution(2185795699286194403)
XLA Ops:
  6.5 0.0 copy-start
  6.5 0.0 reduce-scatter.2.cloned.1.call-start
  6.5 0.0 copy-start.3
  6.5 0.8 fusion.32
  7.4 2.2 fusion
  9.6 0.0 copy-done.3
  9.6 0.0 copy-start.11
  9.6 0.0 copy-start.14
  9.6 2.5 convolution_convert_fusion.4.inner_ref
  12.1 0.0 copy-done.11
  12.2 0.0 copy-done.14
  12.2 0.0 copy-start.4
  12.2 0.0 copy-start.5
  12.2 0.0 copy-start.6
  12.2 0.0 copy-start.7
  12.2 0.0 copy-start.8
  12.2 0.0 copy-start.9
  12.2 0.8 fusion.29.branch_ref
  13.0 0.0 copy-done.4
  13.1 0.1 copy-done.5
  13.1 0.0 copy-done.6
  13.1 0.0 copy-done.7
  13.1 0.0 copy-done.8
  13.1 0.0 copy-done.9
  13.2 13.4 %shard_map.154 = bf16[256,256]{1,0:T(8,128)(2,1)S(1)} custom-call(bf16[256,256]{1,0:T(8,128)(2,1)S(1)} %convolution_convert_fusion.4.inner_ref, f32[256,256]{1,0:T(8,128)S(1)} %fusion.29.branch_ref, f32[4,256]{1,0:T(4,128)S(1)} %copy-done.6, f32[1,256]{1,0:T(1,128)S(1)} %bitcast.21, bf16[1,256,256]{2,1,0:T(8,128)(2,1)S(1)} %copy-done.4, ...), custom_call_target="tpu_custom_call" | custom-call | tf_op jit(solution)/shard_map/pallas_call | solution.py:144
  26.6 0.0 copy-done
  26.6 0.7 convolution_convert_fusion.part_ref
  27.3 110.8 %shard_map.155.base_ref = bf16[256,4096]{1,0:T(8,128)(2,1)S(1)} custom-call(bf16[256,4096]{1,0:T(8,128)(2,1)S(1)} %convolution_convert_fusion.part_ref, bf16[256,4096]{1,0:T(8,128)(2,1)S(1)} %copy-done.3), custom_call_target="tpu_custom_call" | custom-call | tf_op jit(solution)/shard_map/pallas_call | solution.py:314
  138.1 0.0 copy-start.1
  138.2 0.0 copy-start.10
  138.2 0.5 fusion.3
  138.7 0.2 copy-done.10
  138.9 0.6 fusion.5
  139.5 0.0 copy-done.1
  139.6 0.2 copy.20
  139.8 0.0 copy-start.12
  139.8 33.0 %all_to_all.19 = bf16[256,8,512]{2,0,1:T(8,128)(2,1)S(1)} all-to-all(bf16[256,8,512]{2,0,1:T(8,128)(2,1)S(1)} %bitcast.25), channel_id=1, replica_groups=mesh['tp'=16,'seq'=8] {'seq'}, dimensions={1} | all-to-all | bytes 4194304 | tf_op jit(solution)/shard_map/all_to_all | solution.py:368
  172.8 0.0 copy-done.12
  172.8 0.0 copy-start.13
  172.8 1.8 convolution_convert_fusion.2
  174.6 0.0 copy-done.13
  174.6 1.8 convolution_convert_fusion.3
  176.5 3.8 pad_maximum_fusion
  180.3 0.0 reduce-scatter.2.cloned.1.call-update
  180.3 92.4 %reduce-scatter.2.cloned.1.call-done = bf16[256,1536]{0,1:T(8,128)(2,1)} async-done(((bf16[2048,1536]{0,1:T(8,128)(2,1)}), bf16[256,1536]{0,1:T(8,128)(2,1)}) %reduce-scatter.2.cloned.1.call-update) | async-done | bytes 786448 | tf_op jit(solution)/shard_map/reduce_scatter | solution.py:178
  272.7 1.2 convert_element_type.34
  273.9 0.0 copy-start.2
  273.9 4.9 %convolution_convert_fusion.1.part_ref = bf16[256,4096]{1,0:T(8,128)(2,1)S(1)} fusion(bf16[768,4096]{1,0:T(8,128)(2,1)} %param.31, f32[256,1536]{0,1:T(8,128)S(1)} %convert_element_type.34), kind=kOutput, calls=%fused_computation.6 | convolution fusion | flops 1613627392 | bytes 9961472 | tf_op jit(solution)/shard_map/dot_general | solution.py:384
  278.8 0.0 copy-done.2
  278.8 109.0 %shard_map.156 = bf16[256,4096]{1,0:T(8,128)(2,1)S(1)} custom-call(bf16[256,4096]{1,0:T(8,128)(2,1)S(1)} %convolution_convert_fusion.1.part_ref, bf16[256,4096]{1,0:T(8,128)(2,1)S(1)} %copy-done.2), custom_call_target="tpu_custom_call" | custom-call | tf_op jit(solution)/shard_map/pallas_call | solution.py:314
  387.8 1.3 copy.22
  (2 shorter events, 0.0 us)
Async XLA Ops:
  6.5 20.0 %copy-start = (bf16[256,4096]{1,0:T(8,128)(2,1)S(1)}, bf16[256,4096]{1,0:T(8,128)(2,1)}, u32[]{:S(2)}) copy-start(bf16[256,4096]{1,0:T(8,128)(2,1)} %param.27) | copy-start | bytes 6291460
  6.5 266.1 %reduce-scatter.2.cloned.1.call-start = ((), (), s32[]{:S(2)}) async-start(), calls=%async_computation.2 | async-start | bytes 7077888 | tf_op jit(solution)/shard_map/reduce_scatter | solution.py:178
  6.5 3.1 copy-start.3
  9.6 2.5 copy-start.11
  9.6 2.5 copy-start.14
  12.2 0.9 copy-start.4
  12.2 1.0 copy-start.5
  12.2 1.0 copy-start.6
  12.2 0.9 copy-start.7
  12.2 0.9 copy-start.8
  12.2 0.9 copy-start.9
  138.1 1.4 copy-start.1
  138.2 0.7 copy-start.10
  139.8 33.0 %copy-start.12 = (bf16[512,768]{1,0:T(8,128)(2,1)S(1)}, bf16[512,768]{1,0:T(8,128)(2,1)}, u32[]{:S(2)}) copy-start(bf16[512,768]{1,0:T(8,128)(2,1)} %param.30) | copy-start | bytes 2359300
  172.8 1.8 copy-start.13
  273.9 4.9 %copy-start.2 = (bf16[256,4096]{1,0:T(8,128)(2,1)S(1)}, bf16[256,4096]{1,0:T(8,128)(2,1)}, u32[]{:S(2)}) copy-start(bf16[256,4096]{1,0:T(8,128)(2,1)} %copy-done.1) | copy-start | bytes 6291460
Sparse Core Ops, SparseCore 0:
  180.4 92.2 reduce-scatter.1
where the time goes:
time: 396 us
  Pallas kernels  233 us (59%)
  waiting for transfers between devices  92.4 us (23%)
  blocking collectives  33 us (8%)
  between operations  13.6 us (3%)
  matrix products  12.6 us (3%)
  other arithmetic  9.22 us (2%)
    pallas_call x2, Pallas kernels, summed(): pl.pallas_call(functools.partial(summed_kernel, chips), out_shape=jax.Sha...  220 us
    reduce_scatter x1, waiting for transfers between devices, summed_rows(): lax.psum_scatter(everything.astype(jnp.bfloat16), axis, scatter_dimension...  92.4 us
    all_to_all x1, blocking collectives, on_device(): lax.all_to_all(hidden_in, 'seq', split_axis=1, concat_axis=0, tiled=True)  33 us
    pallas_call x1, Pallas kernels, recurrence(): pl.pallas_call(functools.partial(recurrence_kernel, count, conv_weight.sh...  13.4 us
  transfers between devices with their start and end apart: 1, of which 1 were waited for; matrix products, arithmetic and copies ran while one was open for 0% of the time, Pallas kernels for 0%

commit v1 on v0

v1 whole, which is shorter than its diff:
```python
import functools
from types import SimpleNamespace

import jax
import jax.numpy as jnp
from jax import lax
from jax.experimental import pallas as pl
from jax.experimental.pallas import tpu as pltpu
from jax.sharding import PartitionSpec as P

epsilon = 1e-06
LOGICAL = pl.DeviceIdType.MESH
LANES = 128
EDGE = 16


def one_minus_exp(x):
    series = 1.0 + x * (1.0 / 9.0)
    for k in range(8, 1, -1):
        series = 1.0 + x * (1.0 / k) * series
    return jnp.where(x > -0.5, -x * series, 1.0 - jnp.exp(x))


def recurrence_phase(
    count,
    taps,
    me,
    tp,
    inner_ref,
    branch_ref,
    conv_weight_ref,
    conv_bias_ref,
    input_gate_ref,
    input_bias_ref,
    decay_gate_ref,
    decay_bias_ref,
    slope_ref,
    gated_ref,
    tail_ref,
    decays_ref,
    states_ref,
    ends_ref,
    arrived_ref,
    tail_send,
    tail_recv,
    end_send,
    end_recv,
):
    length, channels = inner_ref.shape
    heads, head = input_gate_ref.shape[0], input_gate_ref.shape[1]
    peers = [lax.rem(me + offset, count) for offset in range(1, count)]
    tail_copy = remote(
        inner_ref.at[pl.ds(length - EDGE, EDGE), :], tail_ref, tail_send, tail_recv, tp, peers[0]
    )
    tail_copy.start()
    tail_copy.wait()
    follows = jnp.where(me > 0, 1.0, 0.0)

    for h in range(heads):
        columns = pl.ds(h * head, head)
        row = lax.broadcasted_iota(jnp.int32, (length, head), 0)
        current = inner_ref[:, columns].astype(jnp.float32)
        tail = tail_ref[:, columns].astype(jnp.float32) * follows
        before = jnp.concatenate([tail, jnp.zeros((length - EDGE, head), jnp.float32)], axis=0)
        total = conv_bias_ref[:, columns] + conv_weight_ref[0:1, columns] * current
        for tap in range(1, taps):
            shifted = jnp.where(
                row < tap,
                pltpu.roll(before, length + tap - EDGE, 0),
                pltpu.roll(current, tap, 0),
            )
            total = total + conv_weight_ref[tap : tap + 1, columns] * shifted
        smoothed = total.astype(jnp.bfloat16)
        input_rate = jax.nn.sigmoid(
            jnp.dot(smoothed, input_gate_ref[h], preferred_element_type=jnp.float32)
            + input_bias_ref[:, columns]
        )
        decay_rate = jax.nn.sigmoid(
            jnp.dot(smoothed, decay_gate_ref[h], preferred_element_type=jnp.float32)
            + decay_bias_ref[:, columns]
        )
        log_decay = decay_rate * slope_ref[:, columns]
        scale_in = jnp.sqrt(one_minus_exp(2.0 * log_decay))
        scale_in = jnp.where(jnp.logical_and(row == 0, me == 0), 1.0, scale_in)
        decays_ref[:, columns] = jnp.exp(log_decay)
        states_ref[:, columns] = smoothed.astype(jnp.float32) * input_rate * scale_in

    for c in range(channels // LANES):
        columns = pl.ds(c * LANES, LANES)
        row = lax.broadcasted_iota(jnp.int32, (length, LANES), 0)
        decay, state = decays_ref[:, columns], states_ref[:, columns]
        step = 1
        while step < length:
            reached = row >= step
            state = state + decay * jnp.where(reached, pltpu.roll(state, step, 0), 0.0)
            decay = decay * jnp.where(reached, pltpu.roll(decay, step, 0), 1.0)
            step *= 2
        decays_ref[:, columns] = decay
        states_ref[:, columns] = state
        ends_ref[0:1, columns] = decay[length - 1 :, :]
        ends_ref[1:2, columns] = state[length - 1 :, :]

    copies = [
        remote(ends_ref, arrived_ref.at[k], end_send.at[k], end_recv.at[k], tp, peers[k])
        for k in range(count - 1)
    ]
    for copy in copies:
        copy.start()
    for copy in copies:
        copy.wait()
    carried = jnp.zeros((1, channels), jnp.float32)
    for k in range(count - 2, -1, -1):
        new = arrived_ref[k, 0:1, :] * carried + arrived_ref[k, 1:2, :]
        carried = jnp.where(me >= k + 1, new, carried)
    gated_ref[...] = (
        (states_ref[...] + decays_ref[...] * carried) * branch_ref[...]
    ).astype(jnp.bfloat16)


def remote(source, target, send, recv, tp, seq):
    return pltpu.make_async_remote_copy(
        src_ref=source,
        dst_ref=target,
        send_sem=send,
        recv_sem=recv,
        device_id={"tp": tp, "seq": seq},
        device_id_type=LOGICAL,
    )


def aligned(index, unit):
    return pl.multiple_of(index * unit, unit)


class Links:
    def __init__(self):
        self.t, self.s = lax.axis_index("tp"), lax.axis_index("seq")
        self.core = lax.rem(self.t, 2)
        self.z = lax.rem(lax.div(self.t, 2), 4)
        self.xl = lax.div(self.t, 8)
        self.xh = lax.rem(self.s, 2)
        self.y = lax.div(self.s, 2)
        t, s, y, z, core = self.t, self.s, self.y, self.z, self.core
        x = 2 * self.xh + self.xl

        def along_z(step):
            return (8 * self.xl + 2 * lax.rem(z + step, 4) + core, s)

        def along_y(step):
            return (t, 2 * lax.rem(y + step, 4) + self.xh)

        def along_x(step):
            other = lax.rem(x + step, 4)
            return (8 * lax.rem(other, 2) + 2 * z + core, 2 * y + lax.div(other, 2))

        self.pair = (t + 1 - 2 * core, s)
        self.z_up, self.z_down = along_z(1), along_z(3)
        self.y_up, self.y_down = along_y(1), along_y(3)
        self.x_up, self.x_down = along_x(1), along_x(3)
        self.near = (8 * (1 - self.xl) + 2 * z + core, s)
        self.far = (t, 2 * y + 1 - self.xh)
        self.outside = (8 * (1 - self.xl) + 2 * z + core, lax.select(self.xl == 0, self.x_down[1], self.x_up[1]))
        self.sent = []

    def start(self, source, target, send, recv, device):
        copy = remote(source, target, send, recv, *device)
        copy.start()
        self.sent.append(copy)

    def arrived(self, target, send, recv):
        remote(target, target, send, recv, *self.pair).wait_recv()

    def drain(self):
        for copy in self.sent:
            copy.wait_send()
        self.sent = []


GROUPS = 2


def scatter_scratch(length, width):
    bf = jnp.bfloat16
    rows, unit = length // 8, length // 16
    quarter = width // (2 * GROUPS)
    dma = pltpu.SemaphoreType.DMA
    return dict(
        pair=pltpu.VMEM((4, rows, width), bf),
        out_far=pltpu.VMEM((rows, width), bf),
        out_up=pltpu.VMEM((rows, width), bf),
        out_down=pltpu.VMEM((rows, width), bf),
        far_up=pltpu.VMEM((GROUPS, rows, quarter), bf),
        far_down=pltpu.VMEM((GROUPS, rows, quarter), bf),
        from_down=pltpu.VMEM((2 * GROUPS, rows, quarter), bf),
        from_up=pltpu.VMEM((2 * GROUPS, rows, quarter), bf),
        out_near=pltpu.VMEM((unit, width), bf),
        from_near=pltpu.VMEM((GROUPS, unit, 2 * quarter), bf),
        own=pltpu.VMEM((unit, width), jnp.float32),
        pair_s=dma((4, GROUPS)),
        pair_r=dma((4, GROUPS)),
        far_up_s=dma((GROUPS,)),
        far_up_r=dma((GROUPS,)),
        far_down_s=dma((GROUPS,)),
        far_down_r=dma((GROUPS,)),
        up_s=dma((2 * GROUPS,)),
        up_r=dma((2 * GROUPS,)),
        down_s=dma((2 * GROUPS,)),
        down_r=dma((2 * GROUPS,)),
        near_s=dma((GROUPS,)),
        near_r=dma((GROUPS,)),
    )


def owned_row(links, core, z, xl, unit):
    return aligned(core * 8 + z * 2 + xl, unit)


def pair_up(links, part, b, g):
    rows = b.pair.shape[1]
    width = part.shape[1] // GROUPS
    columns = pl.ds(g * width, width)
    for k, step in enumerate((2, 1, 3, 0)):
        block = (1 - links.core) * 4 + lax.rem(links.z + step, 4)
        links.start(
            part.at[pl.ds(aligned(block, rows), rows), columns],
            b.pair.at[k, :, columns],
            b.pair_s.at[k, g],
            b.pair_r.at[k, g],
            links.pair,
        )


def reduce_scatter(links, part, b, finish):
    rows, width = b.pair.shape[1:]
    unit, quarter = rows // 2, width // (2 * GROUPS)
    order = (2, 1, 3, 0)
    starts = [aligned(links.core * 4 + lax.rem(links.z + step, 4), rows) for step in order]

    def summed(k, q):
        columns = pl.ds(q * quarter, quarter)
        return part[pl.ds(starts[k], rows), columns].astype(jnp.float32) + b.pair[
            k, :, columns
        ].astype(jnp.float32)

    def paired(k, g):
        columns = pl.ds(g * 2 * quarter, 2 * quarter)
        links.arrived(b.pair.at[k, :, columns], b.pair_s.at[k, g], b.pair_r.at[k, g])

    def send_far(g):
        paired(0, g)
        for q, landing, send, recv, device in (
            (2 * g, b.far_up, b.far_up_s, b.far_up_r, links.z_up),
            (2 * g + 1, b.far_down, b.far_down_s, b.far_down_r, links.z_down),
        ):
            columns = pl.ds(q * quarter, quarter)
            b.out_far[:, columns] = summed(0, q).astype(jnp.bfloat16)
            links.start(b.out_far.at[:, columns], landing.at[g], send.at[g], recv.at[g], device)

    def send_up(q, value):
        columns = pl.ds(q * quarter, quarter)
        b.out_up[:, columns] = value.astype(jnp.bfloat16)
        links.start(
            b.out_up.at[:, columns], b.from_down.at[q], b.up_s.at[q], b.up_r.at[q], links.z_up
        )

    def send_down(q, value):
        columns = pl.ds(q * quarter, quarter)
        b.out_down[:, columns] = value.astype(jnp.bfloat16)
        links.start(
            b.out_down.at[:, columns], b.from_up.at[q], b.down_s.at[q], b.down_r.at[q], links.z_down
        )

    def send_first(g):
        paired(1, g)
        send_up(2 * g + 1, summed(1, 2 * g + 1))
        paired(2, g)
        send_down(2 * g, summed(2, 2 * g))

    def send_second(g):
        links.arrived(b.far_up.at[g], b.far_up_s.at[g], b.far_up_r.at[g])
        send_up(2 * g, summed(1, 2 * g) + b.far_up[g].astype(jnp.float32))
        links.arrived(b.far_down.at[g], b.far_down_s.at[g], b.far_down_r.at[g])
        send_down(2 * g + 1, summed(2, 2 * g + 1) + b.far_down[g].astype(jnp.float32))

    def collect(g):
        paired(3, g)
        for q in (2 * g, 2 * g + 1):
            links.arrived(b.from_down.at[q], b.up_s.at[q], b.up_r.at[q])
            links.arrived(b.from_up.at[q], b.down_s.at[q], b.down_r.at[q])
            columns = pl.ds(q * quarter, quarter)
            total = (
                summed(3, q)
                + b.from_down[q].astype(jnp.float32)
                + b.from_up[q].astype(jnp.float32)
            )
            low, high = total[:unit], total[unit:]
            first = links.xl == 0
            b.own[:, columns] = jnp.where(first, low, high)
            b.out_near[:, columns] = jnp.where(first, high, low).astype(jnp.bfloat16)
        columns = pl.ds(g * 2 * quarter, 2 * quarter)
        links.start(
            b.out_near.at[:, columns],
            b.from_near.at[g],
            b.near_s.at[g],
            b.near_r.at[g],
            links.near,
        )

    for g in range(GROUPS):
        send_far(g)
        if g == 0:
            send_first(0)
    for g in range(GROUPS):
        send_second(g)
        if g + 1 < GROUPS:
            send_first(g + 1)
    for g in range(GROUPS):
        collect(g)
    for g in range(GROUPS):
        links.arrived(b.from_near.at[g], b.near_s.at[g], b.near_r.at[g])
        columns = pl.ds(g * 2 * quarter, 2 * quarter)
        finish(columns, b.own[:, columns] + b.from_near[g].astype(jnp.float32))


def gather_scratch():
    dma = pltpu.SemaphoreType.DMA
    return dict(
        near_s=dma((2,)),
        near_r=dma((2,)),
        up_s=dma((2, 2)),
        up_r=dma((2, 2)),
        down_s=dma((2, 2)),
        down_r=dma((2, 2)),
        far_up_s=dma((2, 2)),
        far_up_r=dma((2, 2)),
        far_down_s=dma((2, 2)),
        far_down_r=dma((2, 2)),
        pair_s=dma((2, 10)),
        pair_r=dma((2, 10)),
    )


def all_gather(links, slot, unit, b, ready):
    core, z, xl = links.core, links.z, links.xl

    def row(step, i, c=core):
        across = xl if i == 0 else 1 - xl
        return owned_row(links, c, lax.rem(z + step, 4), across, unit)

    def pass_on(h, n, r, half):
        piece = slot(h, r, half)
        links.start(piece, piece, b.pair_s.at[h, n], b.pair_r.at[h, n], links.pair)

    def send(h, i, r):
        piece = slot(h, r, None)
        links.start(piece, piece, b.up_s.at[h, i], b.up_r.at[h, i], links.z_up)
        links.start(piece, piece, b.down_s.at[h, i], b.down_r.at[h, i], links.z_down)

    for h in range(2):
        ready(h)
        own = row(0, 0)
        piece = slot(h, own, None)
        links.start(piece, piece, b.near_s.at[h], b.near_r.at[h], links.near)
        send(h, 0, own)
        pass_on(h, 0, own, None)
    for h in range(2):
        r = row(0, 1)
        links.arrived(slot(h, r, None), b.near_s.at[h], b.near_r.at[h])
        send(h, 1, r)
        pass_on(h, 1, r, None)
    for i in range(2):
        for h in range(2):
            r = row(3, i)
            links.arrived(slot(h, r, None), b.up_s.at[h, i], b.up_r.at[h, i])
            piece = slot(h, r, 0)
            links.start(piece, piece, b.far_up_s.at[h, i], b.far_up_r.at[h, i], links.z_up)
            pass_on(h, 2 + i, r, None)
            r = row(1, i)
            links.arrived(slot(h, r, None), b.down_s.at[h, i], b.down_r.at[h, i])
            piece = slot(h, r, 1)
            links.start(piece, piece, b.far_down_s.at[h, i], b.far_down_r.at[h, i], links.z_down)
            pass_on(h, 4 + i, r, None)
    for i in range(2):
        for h in range(2):
            r = row(2, i)
            links.arrived(slot(h, r, 0), b.far_up_s.at[h, i], b.far_up_r.at[h, i])
            pass_on(h, 6 + i, r, 0)
            links.arrived(slot(h, r, 1), b.far_down_s.at[h, i], b.far_down_r.at[h, i])
            pass_on(h, 8 + i, r, 1)
    for n, (step, i, half) in enumerate(
        [(0, 0, None), (0, 1, None), (3, 0, None), (3, 1, None), (1, 0, None), (1, 1, None)]
        + [(2, 0, 0), (2, 1, 0), (2, 0, 1), (2, 1, 1)]
    ):
        for h in range(2):
            links.arrived(slot(h, row(step, i, 1 - core), half), b.pair_s.at[h, n], b.pair_r.at[h, n])


PIECE = 256


def layer_kernel(
    count,
    taps,
    inner_ref,
    branch_ref,
    conv_weight_ref,
    conv_bias_ref,
    input_gate_ref,
    input_bias_ref,
    decay_gate_ref,
    decay_bias_ref,
    slope_ref,
    gain_ref,
    residual_ref,
    out_proj_ref,
    gate_proj_ref,
    up_proj_ref,
    down_proj_ref,
    out_ref,
    w,
    first,
    second,
    spread,
    final,
):
    w, first, second, spread, final = (SimpleNamespace(**s) for s in (w, first, second, spread, final))
    links = Links()
    length, width = residual_ref.shape
    depth, hidden_width = gate_proj_ref.shape
    unit = length // 16
    half = width // 2
    everyone = [(links.t, lax.rem(links.s + k, count)) for k in range(1, count)]
    everyone += [links.pair, links.z_up, links.z_down, links.near, links.outside]
    barrier = pltpu.get_barrier_semaphore()
    for tp, seq in everyone:
        pl.semaphore_signal(barrier, inc=1, device_id={"tp": tp, "seq": seq}, device_id_type=LOGICAL)
    own = owned_row(links, links.core, links.z, links.xl, unit)
    depth_of = lambda step: pl.ds(aligned(lax.rem(links.y + step, 4), depth), depth)
    loads = [
        pltpu.make_async_copy(out_proj_ref, w.out_proj, w.load.at[0]),
        pltpu.make_async_copy(residual_ref.at[pl.ds(own, unit), :], w.middle, w.load.at[1]),
        pltpu.make_async_copy(gate_proj_ref, w.gate.at[depth_of(0), :], w.load.at[2]),
        pltpu.make_async_copy(up_proj_ref, w.up.at[depth_of(0), :], w.load.at[3]),
        pltpu.make_async_copy(down_proj_ref, w.down, w.load.at[4]),
    ]
    for load in loads:
        load.start()
    pl.semaphore_wait(barrier, len(everyone))

    mine = depth_of(0)
    for target, source, device, at in (
        (w.gate, gate_proj_ref, links.y_up, 0),
        (w.up, up_proj_ref, links.y_down, 1),
        (w.up, up_proj_ref, links.y_up, 2),
        (w.gate, gate_proj_ref, links.y_down, 3),
    ):
        links.start(source, target.at[mine, :], w.gather_s.at[at], w.gather_r.at[at], device)

    recurrence_phase(
        count,
        taps,
        links.s,
        links.t,
        inner_ref,
        branch_ref,
        conv_weight_ref,
        conv_bias_ref,
        input_gate_ref,
        input_bias_ref,
        decay_gate_ref,
        decay_bias_ref,
        slope_ref,
        w.gated,
        w.tail,
        w.decays,
        w.states,
        w.ends,
        w.arrived,
        w.tail_s,
        w.tail_r,
        w.end_s,
        w.end_r,
    )

    def product(left_ref, right_ref, part_ref, scratch):
        tile = 512
        for g in range(GROUPS):

            def step(i, carry):
                columns = pl.ds(aligned(i, tile), tile)
                part_ref[:, columns] = jnp.dot(
                    left_ref[...], right_ref[:, columns], preferred_element_type=jnp.float32
                ).astype(jnp.bfloat16)
                return carry

            steps = width // (GROUPS * tile)
            lax.fori_loop(g * steps, (g + 1) * steps, step, 0)
            pair_up(links, part_ref, scratch, g)

    loads[0].wait()
    product(w.gated, w.out_proj, w.part, first)
    loads[1].wait()

    def to_middle(columns, total):
        w.middle[:, columns] = (total + w.middle[:, columns].astype(jnp.float32)).astype(jnp.bfloat16)

    reduce_scatter(links, w.part, first, to_middle)

    wide = w.middle[...].astype(jnp.float32)
    factor = lax.rsqrt(jnp.mean(wide * wide, axis=-1, keepdims=True) + epsilon)
    w.normed[...] = (wide * factor * gain_ref[...]).astype(jnp.bfloat16)
    hidden_in = w.hidden_in
    for block in range(4):
        place = pl.ds(block * depth, depth)
        there = pl.ds(aligned(2 * block + 1 - links.xh, depth), depth)
        w.away[:, place] = w.normed[:, there]
    links.start(
        w.away, hidden_in.at[links.xh, pl.ds(own, unit), :], w.far_s.at[0], w.far_r.at[0], links.far
    )
    for block in range(4):
        place = pl.ds(block * depth, depth)
        here = pl.ds(aligned(2 * block + links.xh, depth), depth)
        hidden_in[links.xh, pl.ds(own, unit), place] = w.normed[:, here]

    behind, ahead = depth_of(3), depth_of(1)
    links.arrived(w.gate.at[behind, :], w.gather_s.at[0], w.gather_r.at[0])
    piece = w.gate.at[behind, :]
    links.start(piece, piece, w.gather_s.at[4], w.gather_r.at[4], links.y_up)
    links.arrived(w.up.at[ahead, :], w.gather_s.at[1], w.gather_r.at[1])
    piece = w.up.at[ahead, :]
    links.start(piece, piece, w.gather_s.at[5], w.gather_r.at[5], links.y_down)

    def slot(h, r, side):
        group = links.xh if h == 0 else 1 - links.xh
        columns = pl.ds(0, half) if side is None else pl.ds(side * (half // 2), half // 2)
        return hidden_in.at[group, pl.ds(r, unit), columns]

    def ready(h):
        if h == 1:
            links.arrived(slot(1, own, None), w.far_s.at[0], w.far_r.at[0])

    all_gather(links, slot, unit, spread, ready)

    loads[2].wait()
    loads[3].wait()
    links.arrived(w.up.at[behind, :], w.gather_s.at[2], w.gather_r.at[2])
    links.arrived(w.gate.at[ahead, :], w.gather_s.at[3], w.gather_r.at[3])
    opposite = depth_of(2)
    links.arrived(w.gate.at[opposite, :], w.gather_s.at[4], w.gather_r.at[4])
    links.arrived(w.up.at[opposite, :], w.gather_s.at[5], w.gather_r.at[5])

    pieces = hidden_width // PIECE
    top = length // 2
    sides = ((links.x_up, 0), (links.x_down, 1))
    for j in range(pieces):
        columns = pl.ds(j * PIECE, PIECE)
        left = hidden_in[1 - links.xh]
        for n, weights in enumerate((w.gate, w.up)):
            w.given[j, :, n * PIECE : (n + 1) * PIECE] = jnp.dot(
                left, weights[:, columns], preferred_element_type=jnp.float32
            ).astype(jnp.bfloat16)
        for device, d in sides:
            links.start(
                w.given.at[j, pl.ds(d * top, top), :],
                w.relay.at[d, j],
                w.relay_s.at[d, j],
                w.relay_r.at[d, j],
                device,
            )
    for j in range(pieces):
        columns = pl.ds(j * PIECE, PIECE)
        left = hidden_in[links.xh]
        for n, weights in enumerate((w.gate, w.up)):
            w.kept[j, :, n * PIECE : (n + 1) * PIECE] = jnp.dot(
                left, weights[:, columns], preferred_element_type=jnp.float32
            )
    for j in range(pieces):
        for device, d in sides:
            links.arrived(w.relay.at[d, j], w.relay_s.at[d, j], w.relay_r.at[d, j])
            links.start(
                w.relay.at[d, j], w.taken.at[d, j], w.taken_s.at[d, j], w.taken_r.at[d, j], device
            )
    for j in range(pieces):
        for device, d in sides:
            links.arrived(w.taken.at[d, j], w.taken_s.at[d, j], w.taken_r.at[d, j])
            rows = pl.ds(d * top, top)
            both = w.kept[j, rows, :] + w.taken[d, j].astype(jnp.float32)
            w.hidden[rows, j * PIECE : (j + 1) * PIECE] = (
                jax.nn.gelu(both[:, :PIECE], approximate=True) * both[:, PIECE:]
            ).astype(jnp.bfloat16)

    loads[4].wait()
    product(w.hidden, w.down, w.part2, second)

    def to_out(columns, total):
        out_ref[pl.ds(own, unit), columns] = (
            total + w.middle[:, columns].astype(jnp.float32)
        ).astype(jnp.bfloat16)

    reduce_scatter(links, w.part2, second, to_out)

    def place(h, r, side):
        size = half if side is None else half // 2
        return out_ref.at[pl.ds(r, unit), pl.ds(h * half + (0 if side is None else side * size), size)]

    all_gather(links, place, unit, final, lambda h: None)
    links.drain()


def layer(
    inner,
    branch,
    conv_weight,
    conv_bias,
    input_gate,
    input_bias,
    decay_gate,
    decay_bias,
    slope,
    gain,
    residual,
    out_proj,
    gate_proj,
    up_proj,
    down_proj,
):
    count = lax.axis_size("seq")
    length, channels = inner.shape
    width = residual.shape[1]
    depth, hidden_width = gate_proj.shape
    unit = length // 16
    bf, f32 = jnp.bfloat16, jnp.float32
    dma = pltpu.SemaphoreType.DMA
    vmem = pl.BlockSpec(memory_space=pltpu.VMEM)
    anywhere = pl.BlockSpec(memory_space=pl.ANY)
    pieces = hidden_width // PIECE
    scratch = dict(
        out_proj=pltpu.VMEM(out_proj.shape, bf),
        middle=pltpu.VMEM((unit, width), bf),
        normed=pltpu.VMEM((unit, width), bf),
        away=pltpu.VMEM((unit, width // 2), bf),
        gate=pltpu.VMEM((4 * depth, hidden_width), bf),
        up=pltpu.VMEM((4 * depth, hidden_width), bf),
        down=pltpu.VMEM(down_proj.shape, bf),
        hidden_in=pltpu.VMEM((2, length, width // 2), bf),
        given=pltpu.VMEM((pieces, length, 2 * PIECE), bf),
        kept=pltpu.VMEM((pieces, length, 2 * PIECE), f32),
        relay=pltpu.VMEM((2, pieces, length // 2, 2 * PIECE), bf),
        taken=pltpu.VMEM((2, pieces, length // 2, 2 * PIECE), bf),
        hidden=pltpu.VMEM((length, hidden_width), bf),
        part=pltpu.VMEM((length, width), bf),
        part2=pltpu.VMEM((length, width), bf),
        gated=pltpu.VMEM((length, channels), bf),
        tail=pltpu.VMEM((EDGE, channels), bf),
        decays=pltpu.VMEM((length, channels), f32),
        states=pltpu.VMEM((length, channels), f32),
        ends=pltpu.VMEM((8, channels), f32),
        arrived=pltpu.VMEM((count - 1, 8, channels), f32),
        tail_s=dma,
        tail_r=dma,
        end_s=dma((count - 1,)),
        end_r=dma((count - 1,)),
        load=dma((5,)),
        gather_s=dma((6,)),
        gather_r=dma((6,)),
        far_s=dma((1,)),
        far_r=dma((1,)),
        relay_s=dma((2, pieces)),
        relay_r=dma((2, pieces)),
        taken_s=dma((2, pieces)),
        taken_r=dma((2, pieces)),
    )
    return pl.pallas_call(
        functools.partial(layer_kernel, count, conv_weight.shape[0]),
        out_shape=jax.ShapeDtypeStruct((length, width), bf),
        in_specs=[vmem] * 10 + [anywhere] * 5,
        out_specs=vmem,
        scratch_shapes=(
            scratch,
            scatter_scratch(length, width),
            scatter_scratch(length, width),
            gather_scratch(),
            gather_scratch(),
        ),
        compiler_params=pltpu.CompilerParams(
            collective_id=0, has_side_effects=True, vmem_limit_bytes=56 * 2**20
        ),
    )(
        inner,
        branch,
        conv_weight,
        conv_bias[None],
        input_gate,
        input_bias[None],
        decay_gate,
        decay_bias[None],
        slope[None],
        gain[None],
        residual,
        out_proj,
        gate_proj,
        up_proj,
        down_proj,
    )


def rms_norm(values, gain):
    wide = values.astype(jnp.float32)
    factor = lax.rsqrt(jnp.mean(wide * wide, axis=-1, keepdims=True) + epsilon)
    return (wide * factor * gain).astype(jnp.bfloat16)


def on_device(
    residual,
    mix_gain,
    in_proj,
    branch_proj,
    conv_weight,
    conv_bias,
    input_gate,
    input_bias,
    decay_gate,
    decay_bias,
    decay_param,
    out_proj,
    mlp_gain,
    gate_proj,
    up_proj,
    down_proj,
):
    normed = rms_norm(residual, mix_gain)
    branch = jax.nn.gelu(
        jnp.dot(normed, branch_proj, preferred_element_type=jnp.float32), approximate=True
    )
    inner = jnp.dot(normed, in_proj, preferred_element_type=jnp.float32).astype(jnp.bfloat16)
    return layer(
        inner,
        branch,
        conv_weight,
        conv_bias,
        input_gate,
        input_bias,
        decay_gate,
        decay_bias,
        -8.0 * jax.nn.softplus(decay_param),
        mlp_gain,
        residual,
        out_proj,
        gate_proj,
        up_proj,
        down_proj,
    )


def solution(mesh):
    in_specs = (
        P("seq", None),
        P(),
        P(None, "tp"),
        P(None, "tp"),
        P(None, "tp"),
        P("tp"),
        P("tp", None, None),
        P("tp"),
        P("tp", None, None),
        P("tp"),
        P("tp"),
        P("tp", None),
        P(),
        P("seq", "tp"),
        P("seq", "tp"),
        P("tp", None),
    )
    out_specs = P("seq", None)
    return jax.shard_map(
        on_device, mesh=mesh, in_specs=in_specs, out_specs=out_specs, check_vma=False
    )
```

time: 396 us -> 144 us (0.36)
  Pallas kernels: 233 us -> 134 us
  waiting for transfers between devices: 92.4 us -> 0 us
  blocking collectives: 33 us -> 0 us
  between operations: 13.6 us -> 0.04 us
  matrix products: 12.6 us -> 3.79 us
  other arithmetic: 9.22 us -> 3.5 us
    pallas_call x3 -> x1, Pallas kernels: 233 us -> 134 us  [layer(): pl.pallas_call(functools.partial(layer_kernel, count, conv_weight.shape[0...]
    reduce_scatter x1 -> x0, waiting for transfers between devices: 92.4 us -> none  [summed_rows(): lax.psum_scatter(everything.astype(jnp.bfloat16), axis, scatter_dimension...]
    all_to_all x1 -> x0, blocking collectives: 33 us -> none  [on_device(): lax.all_to_all(hidden_in, 'seq', split_axis=1, concat_axis=0, tiled=True)]
    dot_general x4 -> x0, matrix products: 9.3 us -> none  [the longest x1 4.9 us: on_device(): jnp.dot(hidden, down_proj, preferred_element_type=jnp.float32)]
  transfers between devices with their start and end apart: 1 -> 0, of which waited for: 1 -> 0; matrix products, arithmetic and copies ran while one was open for 0% -> 0% of each run, Pallas kernels for 0% -> 0%
where the time goes in v1:
time: 144 us
  Pallas kernels  134 us (93%)
  matrix products  3.79 us (3%)
  other arithmetic  3.5 us (2%)
  local copies, waits for them, and re-layouts  3.15 us (2%)
    pallas_call x1, Pallas kernels, layer(): pl.pallas_call(functools.partial(layer_kernel, count, conv_weight.shape[0...  134 us
    unnamed x9, local copies, waits for them, and re-layouts  3.15 us

profile of v1, /device:TPU:1, one launch (start us, length us, event | category | flops | bytes accessed | tf_op | source)
XLA Modules:
  0.0 144.1 jit_solution(16739025310155297913)
XLA Ops:
  0.0 0.0 copy-start
  0.0 0.0 copy-start.1
  0.0 1.4 fusion.15
  1.4 2.1 %fusion = f32[256]{0:T(256)S(1)} fusion(bf16[256,4096]{1,0:T(8,128)(2,1)} %residual_ref.1), kind=kLoop, calls=%fused_computation.2 | loop fusion | flops 3145472 | bytes 2098176 | tf_op jit(solution)/shard_map/reduce_sum | solution.py:709
  3.5 0.0 copy-done
  3.5 0.0 copy-done.1
  3.5 0.0 copy-start.2
  3.5 0.0 copy-start.3
  3.6 2.3 %convolution_convert_fusion.inner_ref = bf16[256,256]{1,0:T(8,128)(2,1)} fusion(bf16[4096,256]{1,0:T(8,128)(2,1)S(1)} %copy-done, bf16[256,4096]{1,0:T(8,128)(2,1)S(1)} %copy-done.1, f32[4096]{0:T(1024)} %param.17, f32[256]{0:T(256)S(1)} %add_rsqrt_fusion), kind=kOutput, calls=%fused_computation.5 | convolution fusion | flops 541130752 | bytes 4342784 | tf_op jit(solution)/shard_map/dot_general | solution.py:735
  5.8 0.0 copy-done.2
  5.8 0.0 copy-done.3
  5.9 1.5 %fusion.12.branch_ref = f32[256,256]{1,0:T(8,128)} fusion(bf16[4096,256]{1,0:T(8,128)(2,1)S(1)} %copy-done.2, bf16[256,4096]{1,0:T(8,128)(2,1)S(1)} %copy-done.1, f32[4096]{0:T(1024)S(1)} %copy-done.3, f32[256]{0:T(256)S(1)} %add_rsqrt_fusion), kind=kOutput, calls=%fused_computation.14 | convolution fusion | flops 541589504 | bytes 4473856 | tf_op jit(solution)/shard_map/dot_general | solution.py:733
  7.3 133.6 %shard_map.154 = bf16[256,4096]{1,0:T(8,128)(2,1)} custom-call(bf16[256,256]{1,0:T(8,128)(2,1)} %convolution_convert_fusion.inner_ref, f32[256,256]{1,0:T(8,128)} %fusion.12.branch_ref, f32[4,256]{1,0:T(4,128)} %conv_weight_ref.1, f32[1,256]{1,0:T(1,128)} %bitcast.9, bf16[1,256,256]{2,1,0:T(8,128)(2,1)} %input_gate_ref.1, f32[1,256]{1,0:T(1,128)} %bitcast.10, ...), custom_call_target="tpu_custom_call" | custom-call | tf_op jit(solution)/shard_map/pallas_call | solution.py:673
  140.9 3.1 %copy.18 = bf16[256,4096]{1,0:T(8,128)(2,1)} copy(bf16[256,4096]{1,0:T(8,128)(2,1)} %shard_map.154) | data formatting | bytes 4194304
  (1 shorter events, 0.0 us)
Async XLA Ops:
  0.0 3.5 %copy-start = (bf16[4096,256]{1,0:T(8,128)(2,1)S(1)}, bf16[4096,256]{1,0:T(8,128)(2,1)}, u32[]{:S(2)}) copy-start(bf16[4096,256]{1,0:T(8,128)(2,1)} %param.18) | copy-start | bytes 6291460
  0.0 3.5 %copy-start.1 = (bf16[256,4096]{1,0:T(8,128)(2,1)S(1)}, bf16[256,4096]{1,0:T(8,128)(2,1)}, u32[]{:S(2)}) copy-start(bf16[256,4096]{1,0:T(8,128)(2,1)} %residual_ref.1) | copy-start | bytes 6291460
  3.5 2.3 %copy-start.2 = (bf16[4096,256]{1,0:T(8,128)(2,1)S(1)}, bf16[4096,256]{1,0:T(8,128)(2,1)}, u32[]{:S(2)}) copy-start(bf16[4096,256]{1,0:T(8,128)(2,1)} %param.19) | copy-start | bytes 6291460
  3.5 2.3 %copy-start.3 = (f32[4096]{0:T(1024)S(1)}, f32[4096]{0:T(1024)}, u32[]{:S(2)}) copy-start(f32[4096]{0:T(1024)} %param.17) | copy-start | bytes 49156

commit v2 on v1

--- a/solution.py
+++ b/solution.py
@@ -11,7 +11,8 @@
 epsilon = 1e-06
 LOGICAL = pl.DeviceIdType.MESH
 LANES = 128
-EDGE = 16
+EDGE = 8
+GRANT = 44 * 2**20
 
 
 def one_minus_exp(x):
@@ -21,46 +22,37 @@
     return jnp.where(x > -0.5, -x * series, 1.0 - jnp.exp(x))
 
 
-def recurrence_phase(
-    count,
+def softplus(v):
+    small = jnp.exp(-jnp.abs(v))
+    whole = 1.0 + small
+    grown = jnp.where(whole == 1.0, small, jnp.log(whole) * small / jnp.where(whole == 1.0, 1.0, whole - 1.0))
+    return jnp.maximum(v, 0.0) + grown
+
+
+def local_states(
     taps,
     me,
-    tp,
     inner_ref,
-    branch_ref,
     conv_weight_ref,
     conv_bias_ref,
     input_gate_ref,
     input_bias_ref,
     decay_gate_ref,
     decay_bias_ref,
-    slope_ref,
-    gated_ref,
-    tail_ref,
+    decay_param_ref,
     decays_ref,
     states_ref,
     ends_ref,
-    arrived_ref,
-    tail_send,
-    tail_recv,
-    end_send,
-    end_recv,
 ):
-    length, channels = inner_ref.shape
+    length, channels = inner_ref.shape[0] - EDGE, inner_ref.shape[1]
     heads, head = input_gate_ref.shape[0], input_gate_ref.shape[1]
-    peers = [lax.rem(me + offset, count) for offset in range(1, count)]
-    tail_copy = remote(
-        inner_ref.at[pl.ds(length - EDGE, EDGE), :], tail_ref, tail_send, tail_recv, tp, peers[0]
-    )
-    tail_copy.start()
-    tail_copy.wait()
     follows = jnp.where(me > 0, 1.0, 0.0)
 
     for h in range(heads):
         columns = pl.ds(h * head, head)
         row = lax.broadcasted_iota(jnp.int32, (length, head), 0)
-        current = inner_ref[:, columns].astype(jnp.float32)
-        tail = tail_ref[:, columns].astype(jnp.float32) * follows
+        current = inner_ref[:length, columns].astype(jnp.float32)
+        tail = inner_ref[length:, columns].astype(jnp.float32) * follows
         before = jnp.concatenate([tail, jnp.zeros((length - EDGE, head), jnp.float32)], axis=0)
         total = conv_bias_ref[:, columns] + conv_weight_ref[0:1, columns] * current
         for tap in range(1, taps):
@@ -79,7 +71,7 @@
             jnp.dot(smoothed, decay_gate_ref[h], preferred_element_type=jnp.float32)
             + decay_bias_ref[:, columns]
         )
-        log_decay = decay_rate * slope_ref[:, columns]
+        log_decay = decay_rate * (-8.0 * softplus(decay_param_ref[:, columns]))
         scale_in = jnp.sqrt(one_minus_exp(2.0 * log_decay))
         scale_in = jnp.where(jnp.logical_and(row == 0, me == 0), 1.0, scale_in)
         decays_ref[:, columns] = jnp.exp(log_decay)
@@ -99,22 +91,6 @@
         states_ref[:, columns] = state
         ends_ref[0:1, columns] = decay[length - 1 :, :]
         ends_ref[1:2, columns] = state[length - 1 :, :]
-
-    copies = [
-        remote(ends_ref, arrived_ref.at[k], end_send.at[k], end_recv.at[k], tp, peers[k])
-        for k in range(count - 1)
-    ]
-    for copy in copies:
-        copy.start()
-    for copy in copies:
-        copy.wait()
-    carried = jnp.zeros((1, channels), jnp.float32)
-    for k in range(count - 2, -1, -1):
-        new = arrived_ref[k, 0:1, :] * carried + arrived_ref[k, 1:2, :]
-        carried = jnp.where(me >= k + 1, new, carried)
-    gated_ref[...] = (
-        (states_ref[...] + decays_ref[...] * carried) * branch_ref[...]
-    ).astype(jnp.bfloat16)
 
 
 def remote(source, target, send, recv, tp, seq):
@@ -398,89 +374,145 @@
 PIECE = 256
 
 
+CHUNKS = 4
+
+
 def layer_kernel(
     count,
     taps,
-    inner_ref,
-    branch_ref,
-    conv_weight_ref,
-    conv_bias_ref,
-    input_gate_ref,
-    input_bias_ref,
-    decay_gate_ref,
-    decay_bias_ref,
-    slope_ref,
-    gain_ref,
-    residual_ref,
-    out_proj_ref,
-    gate_proj_ref,
-    up_proj_ref,
-    down_proj_ref,
-    out_ref,
-    w,
-    first,
-    second,
-    spread,
-    final,
+    *refs,
 ):
+    outside, (out_ref, w, first, second, spread, final) = refs[:9], refs[16:]
+    residual_ref, in_proj_ref, branch_proj_ref, out_proj_ref, gate_proj_ref, up_proj_ref, down_proj_ref = refs[9:16]
     w, first, second, spread, final = (SimpleNamespace(**s) for s in (w, first, second, spread, final))
     links = Links()
     length, width = residual_ref.shape
     depth, hidden_width = gate_proj_ref.shape
     unit = length // 16
     half = width // 2
-    everyone = [(links.t, lax.rem(links.s + k, count)) for k in range(1, count)]
-    everyone += [links.pair, links.z_up, links.z_down, links.near, links.outside]
+    peers = [(links.t, lax.rem(links.s + k, count)) for k in range(1, count)]
+    everyone = peers + [links.pair, links.z_up, links.z_down, links.near, links.outside]
     barrier = pltpu.get_barrier_semaphore()
     for tp, seq in everyone:
         pl.semaphore_signal(barrier, inc=1, device_id={"tp": tp, "seq": seq}, device_id_type=LOGICAL)
     own = owned_row(links, links.core, links.z, links.xl, unit)
-    depth_of = lambda step: pl.ds(aligned(lax.rem(links.y + step, 4), depth), depth)
+
+    behind, here, ahead, opposite = (p * depth for p in range(4))
     loads = [
-        pltpu.make_async_copy(out_proj_ref, w.out_proj, w.load.at[0]),
-        pltpu.make_async_copy(residual_ref.at[pl.ds(own, unit), :], w.middle, w.load.at[1]),
-        pltpu.make_async_copy(gate_proj_ref, w.gate.at[depth_of(0), :], w.load.at[2]),
-        pltpu.make_async_copy(up_proj_ref, w.up.at[depth_of(0), :], w.load.at[3]),
-        pltpu.make_async_copy(down_proj_ref, w.down, w.load.at[4]),
+        pltpu.make_async_copy(residual_ref, w.normed.at[pl.ds(0, length), :], w.load.at[0]),
+        pltpu.make_async_copy(in_proj_ref, w.in_proj, w.load.at[1]),
+        pltpu.make_async_copy(branch_proj_ref, w.branch_proj, w.load.at[2]),
+        pltpu.make_async_copy(out_proj_ref, w.out_proj, w.load.at[3]),
+        pltpu.make_async_copy(residual_ref.at[pl.ds(own, unit), :], w.middle, w.load.at[4]),
+        pltpu.make_async_copy(gate_proj_ref, w.gate.at[pl.ds(here, depth), :], w.load.at[5]),
+        pltpu.make_async_copy(up_proj_ref, w.up.at[pl.ds(here, depth), :], w.load.at[6]),
+        pltpu.make_async_copy(down_proj_ref, w.down, w.load.at[7]),
     ]
-    for load in loads:
+    small_loads = [
+        pltpu.make_async_copy(source, target, w.small_load.at[k])
+        for k, (source, target) in enumerate(zip(outside, w.small))
+    ]
+    for load in loads[:2] + small_loads + loads[2:3]:
         load.start()
-    pl.semaphore_wait(barrier, len(everyone))
-
-    mine = depth_of(0)
-    for target, source, device, at in (
-        (w.gate, gate_proj_ref, links.y_up, 0),
-        (w.up, up_proj_ref, links.y_down, 1),
-        (w.up, up_proj_ref, links.y_up, 2),
-        (w.gate, gate_proj_ref, links.y_down, 3),
-    ):
-        links.start(source, target.at[mine, :], w.gather_s.at[at], w.gather_r.at[at], device)
-
-    recurrence_phase(
-        count,
-        taps,
-        links.s,
-        links.t,
-        inner_ref,
-        branch_ref,
+    (
+        mix_gain_ref,
         conv_weight_ref,
         conv_bias_ref,
         input_gate_ref,
         input_bias_ref,
         decay_gate_ref,
         decay_bias_ref,
-        slope_ref,
-        w.gated,
-        w.tail,
+        decay_param_ref,
+        gain_ref,
+    ) = w.small
+    pl.semaphore_wait(barrier, len(everyone))
+
+    edge = pl.ds(length, EDGE)
+    links.start(
+        residual_ref.at[pl.ds(length - EDGE, EDGE), :], w.normed.at[edge, :], w.tail_s, w.tail_r, peers[0]
+    )
+    share = depth // CHUNKS
+
+    def gather(n):
+        rows = pl.ds(n % CHUNKS * share, share)
+        sides = ((gate_proj_ref, w.gate), (up_proj_ref, w.up))
+        for d, device in enumerate((links.y_up, links.y_down)):
+            source, target = sides[(n // CHUNKS + d) % 2]
+            there = pl.ds((ahead if d else behind) + n % CHUNKS * share, share)
+            links.start(
+                source.at[rows, :], target.at[there, :], w.gather_s.at[d, n], w.gather_r.at[d, n], device
+            )
+
+    def gathered(d, n):
+        target = (w.gate, w.up)[(n // CHUNKS + d) % 2] if n < 2 * CHUNKS else (w.gate, w.up)[d]
+        start = (ahead if d else behind) if n < 2 * CHUNKS else opposite
+        piece = target.at[pl.ds(start + n % CHUNKS * share, share), :]
+        links.arrived(piece, w.gather_s.at[d, n], w.gather_r.at[d, n])
+        return target
+
+    def forward(n):
+        for d, device in enumerate((links.y_up, links.y_down)):
+            target = gathered(d, n)
+            source = pl.ds((ahead if d else behind) + n * share, share)
+            there = pl.ds(opposite + n * share, share)
+            at = 2 * CHUNKS + n
+            links.start(
+                target.at[source, :], target.at[there, :], w.gather_s.at[d, at], w.gather_r.at[d, at], device
+            )
+
+    gather(0)
+    for load in loads[3:]:
+        load.start()
+
+    def norm(start, rows):
+        place = pl.ds(start, rows)
+        wide = w.normed[place, :].astype(jnp.float32)
+        factor = lax.rsqrt(jnp.mean(wide * wide, axis=-1, keepdims=True) + epsilon)
+        w.normed[place, :] = (wide * factor * mix_gain_ref[...]).astype(jnp.bfloat16)
+
+    def norm_step(i, carry):
+        norm(aligned(i, unit), unit)
+        return carry
+
+    for load in small_loads:
+        load.wait()
+    loads[0].wait()
+    lax.fori_loop(0, 16, norm_step, 0)
+    links.arrived(w.normed.at[edge, :], w.tail_s, w.tail_r)
+    norm(length, EDGE)
+    loads[1].wait()
+    w.inner[...] = jnp.dot(w.normed[...], w.in_proj[...], preferred_element_type=jnp.float32).astype(
+        jnp.bfloat16
+    )
+    local_states(
+        taps,
+        links.s,
+        w.inner,
+        conv_weight_ref,
+        conv_bias_ref,
+        input_gate_ref,
+        input_bias_ref,
+        decay_gate_ref,
+        decay_bias_ref,
+        decay_param_ref,
         w.decays,
         w.states,
         w.ends,
-        w.arrived,
-        w.tail_s,
-        w.tail_r,
-        w.end_s,
-        w.end_r,
-    )
+    )
+    for k in range(count - 1):
+        links.start(w.ends, w.arrived.at[k], w.end_s.at[k], w.end_r.at[k], peers[k])
+    for n in range(1, 2 * CHUNKS):
+        gather(n)
+    loads[2].wait()
+    branch = jax.nn.gelu(
+        jnp.dot(w.normed[:length, :], w.branch_proj[...], preferred_element_type=jnp.float32), approximate=True
+    )
+    carried = jnp.zeros((1, w.ends.shape[1]), jnp.float32)
+    for k in range(count - 2, -1, -1):
+        links.arrived(w.arrived.at[k], w.end_s.at[k], w.end_r.at[k])
+        new = w.arrived[k, 0:1, :] * carried + w.arrived[k, 1:2, :]
+        carried = jnp.where(links.s >= k + 1, new, carried)
+    w.gated[...] = ((w.states[...] + w.decays[...] * carried) * branch).astype(jnp.bfloat16)
 
     def product(left_ref, right_ref, part_ref, scratch):
         tile = 512
@@ -497,9 +529,9 @@
             lax.fori_loop(g * steps, (g + 1) * steps, step, 0)
             pair_up(links, part_ref, scratch, g)
 
-    loads[0].wait()
+    loads[3].wait()
     product(w.gated, w.out_proj, w.part, first)
-    loads[1].wait()
+    loads[4].wait()
 
     def to_middle(columns, total):
         w.middle[:, columns] = (total + w.middle[:, columns].astype(jnp.float32)).astype(jnp.bfloat16)
@@ -508,27 +540,21 @@
 
     wide = w.middle[...].astype(jnp.float32)
     factor = lax.rsqrt(jnp.mean(wide * wide, axis=-1, keepdims=True) + epsilon)
-    w.normed[...] = (wide * factor * gain_ref[...]).astype(jnp.bfloat16)
+    w.chosen[...] = (wide * factor * gain_ref[...]).astype(jnp.bfloat16)
     hidden_in = w.hidden_in
-    for block in range(4):
-        place = pl.ds(block * depth, depth)
-        there = pl.ds(aligned(2 * block + 1 - links.xh, depth), depth)
-        w.away[:, place] = w.normed[:, there]
+
+    def features(p, which):
+        return pl.ds(aligned(2 * lax.rem(links.y + 3 + p, 4) + which, depth), depth)
+
+    for p in range(4):
+        w.away[:, p * depth : (p + 1) * depth] = w.chosen[:, features(p, 1 - links.xh)]
     links.start(
         w.away, hidden_in.at[links.xh, pl.ds(own, unit), :], w.far_s.at[0], w.far_r.at[0], links.far
     )
-    for block in range(4):
-        place = pl.ds(block * depth, depth)
-        here = pl.ds(aligned(2 * block + links.xh, depth), depth)
-        hidden_in[links.xh, pl.ds(own, unit), place] = w.normed[:, here]
-
-    behind, ahead = depth_of(3), depth_of(1)
-    links.arrived(w.gate.at[behind, :], w.gather_s.at[0], w.gather_r.at[0])
-    piece = w.gate.at[behind, :]
-    links.start(piece, piece, w.gather_s.at[4], w.gather_r.at[4], links.y_up)
-    links.arrived(w.up.at[ahead, :], w.gather_s.at[1], w.gather_r.at[1])
-    piece = w.up.at[ahead, :]
-    links.start(piece, piece, w.gather_s.at[5], w.gather_r.at[5], links.y_down)
+    for p in range(4):
+        hidden_in[links.xh, pl.ds(own, unit), p * depth : (p + 1) * depth] = w.chosen[:, features(p, links.xh)]
+    for n in range(CHUNKS):
+        forward(n)
 
     def slot(h, r, side):
         group = links.xh if h == 0 else 1 - links.xh
@@ -541,24 +567,39 @@
 
     all_gather(links, slot, unit, spread, ready)
 
-    loads[2].wait()
-    loads[3].wait()
-    links.arrived(w.up.at[behind, :], w.gather_s.at[2], w.gather_r.at[2])
-    links.arrived(w.gate.at[ahead, :], w.gather_s.at[3], w.gather_r.at[3])
-    opposite = depth_of(2)
-    links.arrived(w.gate.at[opposite, :], w.gather_s.at[4], w.gather_r.at[4])
-    links.arrived(w.up.at[opposite, :], w.gather_s.at[5], w.gather_r.at[5])
+    loads[5].wait()
+    loads[6].wait()
+    for n in range(CHUNKS, 2 * CHUNKS):
+        for d in range(2):
+            gathered(d, n)
 
     pieces = hidden_width // PIECE
     top = length // 2
     sides = ((links.x_up, 0), (links.x_down, 1))
+
+    def partial(group, j, place):
+        return jnp.concatenate(
+            [
+                jnp.dot(
+                    hidden_in[group, :, place],
+                    weights[place, j * PIECE : (j + 1) * PIECE],
+                    preferred_element_type=jnp.float32,
+                )
+                for weights in (w.gate, w.up)
+            ],
+            axis=1,
+        )
+
+    nearby, distant = pl.ds(0, opposite), pl.ds(opposite, depth)
     for j in range(pieces):
-        columns = pl.ds(j * PIECE, PIECE)
-        left = hidden_in[1 - links.xh]
-        for n, weights in enumerate((w.gate, w.up)):
-            w.given[j, :, n * PIECE : (n + 1) * PIECE] = jnp.dot(
-                left, weights[:, columns], preferred_element_type=jnp.float32
-            ).astype(jnp.bfloat16)
+        w.lent[j] = partial(1 - links.xh, j, nearby)
+    for j in range(pieces):
+        w.kept[j] = partial(links.xh, j, nearby)
+    for n in range(CHUNKS):
+        for d in range(2):
+            gathered(d, 2 * CHUNKS + n)
+    for j in range(pieces):
+        w.given[j] = (w.lent[j] + partial(1 - links.xh, j, distant)).astype(jnp.bfloat16)
         for device, d in sides:
             links.start(
                 w.given.at[j, pl.ds(d * top, top), :],
@@ -568,12 +609,7 @@
                 device,
             )
     for j in range(pieces):
-        columns = pl.ds(j * PIECE, PIECE)
-        left = hidden_in[links.xh]
-        for n, weights in enumerate((w.gate, w.up)):
-            w.kept[j, :, n * PIECE : (n + 1) * PIECE] = jnp.dot(
-                left, weights[:, columns], preferred_element_type=jnp.float32
-            )
+        w.kept[j] += partial(links.xh, j, distant)
     for j in range(pieces):
         for device, d in sides:
             links.arrived(w.relay.at[d, j], w.relay_s.at[d, j], w.relay_r.at[d, j])
@@ -589,7 +625,7 @@
                 jax.nn.gelu(both[:, :PIECE], approximate=True) * both[:, PIECE:]
             ).astype(jnp.bfloat16)
 
-    loads[4].wait()
+    loads[7].wait()
     product(w.hidden, w.down, w.part2, second)
 
     def to_out(columns, total):
@@ -605,109 +641,6 @@
 
     all_gather(links, place, unit, final, lambda h: None)
     links.drain()
-
-
-def layer(
-    inner,
-    branch,
-    conv_weight,
-    conv_bias,
-    input_gate,
-    input_bias,
-    decay_gate,
-    decay_bias,
-    slope,
-    gain,
-    residual,
-    out_proj,
-    gate_proj,
-    up_proj,
-    down_proj,
-):
-    count = lax.axis_size("seq")
-    length, channels = inner.shape
-    width = residual.shape[1]
-    depth, hidden_width = gate_proj.shape
-    unit = length // 16
-    bf, f32 = jnp.bfloat16, jnp.float32
-    dma = pltpu.SemaphoreType.DMA
-    vmem = pl.BlockSpec(memory_space=pltpu.VMEM)
-    anywhere = pl.BlockSpec(memory_space=pl.ANY)
-    pieces = hidden_width // PIECE
-    scratch = dict(
-        out_proj=pltpu.VMEM(out_proj.shape, bf),
-        middle=pltpu.VMEM((unit, width), bf),
-        normed=pltpu.VMEM((unit, width), bf),
-        away=pltpu.VMEM((unit, width // 2), bf),
-        gate=pltpu.VMEM((4 * depth, hidden_width), bf),
-        up=pltpu.VMEM((4 * depth, hidden_width), bf),
-        down=pltpu.VMEM(down_proj.shape, bf),
-        hidden_in=pltpu.VMEM((2, length, width // 2), bf),
-        given=pltpu.VMEM((pieces, length, 2 * PIECE), bf),
-        kept=pltpu.VMEM((pieces, length, 2 * PIECE), f32),
-        relay=pltpu.VMEM((2, pieces, length // 2, 2 * PIECE), bf),
-        taken=pltpu.VMEM((2, pieces, length // 2, 2 * PIECE), bf),
-        hidden=pltpu.VMEM((length, hidden_width), bf),
-        part=pltpu.VMEM((length, width), bf),
-        part2=pltpu.VMEM((length, width), bf),
-        gated=pltpu.VMEM((length, channels), bf),
-        tail=pltpu.VMEM((EDGE, channels), bf),
-        decays=pltpu.VMEM((length, channels), f32),
-        states=pltpu.VMEM((length, channels), f32),
-        ends=pltpu.VMEM((8, channels), f32),
-        arrived=pltpu.VMEM((count - 1, 8, channels), f32),
-        tail_s=dma,
-        tail_r=dma,
-        end_s=dma((count - 1,)),
-        end_r=dma((count - 1,)),
-        load=dma((5,)),
-        gather_s=dma((6,)),
-        gather_r=dma((6,)),
-        far_s=dma((1,)),
-        far_r=dma((1,)),
-        relay_s=dma((2, pieces)),
-        relay_r=dma((2, pieces)),
-        taken_s=dma((2, pieces)),
-        taken_r=dma((2, pieces)),
-    )
-    return pl.pallas_call(
-        functools.partial(layer_kernel, count, conv_weight.shape[0]),
-        out_shape=jax.ShapeDtypeStruct((length, width), bf),
-        in_specs=[vmem] * 10 + [anywhere] * 5,
-        out_specs=vmem,
-        scratch_shapes=(
-            scratch,
-            scatter_scratch(length, width),
-            scatter_scratch(length, width),
-            gather_scratch(),
-            gather_scratch(),
-        ),
-        compiler_params=pltpu.CompilerParams(
-            collective_id=0, has_side_effects=True, vmem_limit_bytes=56 * 2**20
-        ),
-    )(
-        inner,
-        branch,
-        conv_weight,
-        conv_bias[None],
-        input_gate,
-        input_bias[None],
-        decay_gate,
-        decay_bias[None],
-        slope[None],
-        gain[None],
-        residual,
-        out_proj,
-        gate_proj,
-        up_proj,
-        down_proj,
-    )
-
-
-def rms_norm(values, gain):
-    wide = values.astype(jnp.float32)
-    factor = lax.rsqrt(jnp.mean(wide * wide, axis=-1, keepdims=True) + epsilon)
-    return (wide * factor * gain).astype(jnp.bfloat16)
 
 
 def on_device(
@@ -728,27 +661,97 @@
     up_proj,
     down_proj,
 ):
-    normed = rms_norm(residual, mix_gain)
-    branch = jax.nn.gelu(
-        jnp.dot(normed, branch_proj, preferred_element_type=jnp.float32), approximate=True
-    )
-    inner = jnp.dot(normed, in_proj, preferred_element_type=jnp.float32).astype(jnp.bfloat16)
-    return layer(
-        inner,
-        branch,
+    count = lax.axis_size("seq")
+    length, width = residual.shape
+    channels = in_proj.shape[1]
+    depth, hidden_width = gate_proj.shape
+    unit = length // 16
+    bf, f32 = jnp.bfloat16, jnp.float32
+    dma = pltpu.SemaphoreType.DMA
+    outer = pl.BlockSpec(memory_space=pltpu.HBM)
+    pieces = hidden_width // PIECE
+    small = (
+        mix_gain[None],
         conv_weight,
-        conv_bias,
+        conv_bias[None],
         input_gate,
-        input_bias,
+        input_bias[None],
         decay_gate,
-        decay_bias,
-        -8.0 * jax.nn.softplus(decay_param),
-        mlp_gain,
-        residual,
-        out_proj,
-        gate_proj,
-        up_proj,
-        down_proj,
+        decay_bias[None],
+        decay_param[None],
+        mlp_gain[None],
+    )
+    scratch = dict(
+        small=tuple(pltpu.VMEM(array.shape, array.dtype) for array in small),
+        small_load=dma((len(small),)),
+        normed=pltpu.VMEM((length + EDGE, width), bf),
+        in_proj=pltpu.VMEM(in_proj.shape, bf),
+        branch_proj=pltpu.VMEM(branch_proj.shape, bf),
+        inner=pltpu.VMEM((length + EDGE, channels), bf),
+        out_proj=pltpu.VMEM(out_proj.shape, bf),
+        middle=pltpu.VMEM((unit, width), bf),
+        chosen=pltpu.VMEM((unit, width), bf),
+        away=pltpu.VMEM((unit, width // 2), bf),
+        gate=pltpu.VMEM((4 * depth, hidden_width), bf),
+        up=pltpu.VMEM((4 * depth, hidden_width), bf),
+        down=pltpu.VMEM(down_proj.shape, bf),
+        hidden_in=pltpu.VMEM((2, length, width // 2), bf),
+        given=pltpu.VMEM((pieces, length, 2 * PIECE), bf),
+        lent=pltpu.VMEM((pieces, length, 2 * PIECE), f32),
+        kept=pltpu.VMEM((pieces, length, 2 * PIECE), f32),
+        relay=pltpu.VMEM((2, pieces, length // 2, 2 * PIECE), bf),
+        taken=pltpu.VMEM((2, pieces, length // 2, 2 * PIECE), bf),
+        hidden=pltpu.VMEM((length, hidden_width), bf),
+        part=pltpu.VMEM((length, width), bf),
+        part2=pltpu.VMEM((length, width), bf),
+        gated=pltpu.VMEM((length, channels), bf),
+        decays=pltpu.VMEM((length, channels), f32),
+        states=pltpu.VMEM((length, channels), f32),
+        ends=pltpu.VMEM((8, channels), f32),
+        arrived=pltpu.VMEM((count - 1, 8, channels), f32),
+        tail_s=dma,
+        tail_r=dma,
+        end_s=dma((count - 1,)),
+        end_r=dma((count - 1,)),
+        load=dma((8,)),
+        gather_s=dma((2, 3 * CHUNKS)),
+        gather_r=dma((2, 3 * CHUNKS)),
+        far_s=dma((1,)),
+        far_r=dma((1,)),
+        relay_s=dma((2, pieces)),
+        relay_r=dma((2, pieces)),
+        taken_s=dma((2, pieces)),
+        taken_r=dma((2, pieces)),
+    )
+    return pl.pallas_call(
+        functools.partial(layer_kernel, count, conv_weight.shape[0]),
+        out_shape=jax.ShapeDtypeStruct((length, width), bf),
+        in_specs=[outer] * 16,
+        out_specs=pl.BlockSpec(memory_space=pltpu.VMEM),
+        scratch_shapes=(
+            scratch,
+            scatter_scratch(length, width),
+            scatter_scratch(length, width),
+            gather_scratch(),
+            gather_scratch(),
+        ),
+        compiler_params=pltpu.CompilerParams(
+            collective_id=0, has_side_effects=True, vmem_limit_bytes=GRANT
+        ),
+    )(
+        *(
+            pltpu.with_memory_space_constraint(array, pltpu.HBM)
+            for array in (
+                *small,
+                residual,
+                in_proj,
+                branch_proj,
+                out_proj,
+                gate_proj,
+                up_proj,
+                down_proj,
+            )
+        )
     )
 
 

time: 144 us -> 116 us (0.81)
  Pallas kernels: 134 us -> 114 us
  matrix products: 3.79 us -> 0 us
  other arithmetic: 3.5 us -> 0 us
  local copies, waits for them, and re-layouts: 3.15 us -> 1.32 us
    pallas_call x1, Pallas kernels: 134 us -> 114 us  [on_device(): pl.pallas_call(functools.partial(layer_kernel, count, conv_weight.shape[0...]
    dot_general x2 -> x0, matrix products: 3.79 us -> none  [the longest x1 2.29 us: on_device(): jnp.dot(normed, in_proj, preferred_element_type=jnp.float32)]
    reduce_sum x1 -> x0, other arithmetic: 2.08 us -> none  [rms_norm(): factor = lax.rsqrt(jnp.mean(wide * wide, axis=-1, keepdims=True) + epsilon)]
    unnamed x9 -> x1, local copies, waits for them, and re-layouts: 3.15 us -> 1.32 us
where the time goes in v2:
time: 116 us
  Pallas kernels  114 us (98%)
  local copies, waits for them, and re-layouts  1.32 us (1%)
    pallas_call x1, Pallas kernels, on_device(): pl.pallas_call(functools.partial(layer_kernel, count, conv_weight.shape[0...  114 us

profile of v2, /device:TPU:1, one launch (start us, length us, event | category | flops | bytes accessed | tf_op | source)
XLA Modules:
  0.0 115.6 jit_solution(11426742592097782702)
XLA Ops:
  0.0 114.3 %shard_map.154 = bf16[256,4096]{1,0:T(8,128)(2,1)S(1)} custom-call(f32[1,4096]{1,0:T(1,128)} %bitcast.6, f32[4,256]{1,0:T(4,128)} %refs_1_.1, f32[1,256]{1,0:T(1,128)} %bitcast.8, bf16[1,256,256]{2,1,0:T(8,128)(2,1)} %refs_3_.1, f32[1,256]{1,0:T(1,128)} %bitcast.9, bf16[1,256,256]{2,1,0:T(8,128)(2,1)} %refs_5_.1, f32[1,256]{1,0:T(1,128)} %bitcast.10, ...), custom_call_target="tpu_custom_call" | custom-call | tf_op jit(solution)/shard_map/pallas_call | solution.py:726
  114.3 1.3 %copy.18 = bf16[256,4096]{1,0:T(8,128)(2,1)} copy(bf16[256,4096]{1,0:T(8,128)(2,1)S(1)} %shard_map.154) | data formatting | bytes 4194304

commit v3 on v2

--- a/solution.py
+++ b/solution.py
@@ -12,7 +12,7 @@
 LOGICAL = pl.DeviceIdType.MESH
 LANES = 128
 EDGE = 8
-GRANT = 44 * 2**20
+GRANT = 50 * 2**20
 
 
 def one_minus_exp(x):
@@ -371,7 +371,7 @@
             links.arrived(slot(h, row(step, i, 1 - core), half), b.pair_s.at[h, n], b.pair_r.at[h, n])
 
 
-PIECE = 256
+PIECE = 128
 
 
 CHUNKS = 4
@@ -444,21 +444,28 @@
             )
 
     def gathered(d, n):
-        target = (w.gate, w.up)[(n // CHUNKS + d) % 2] if n < 2 * CHUNKS else (w.gate, w.up)[d]
-        start = (ahead if d else behind) if n < 2 * CHUNKS else opposite
-        piece = target.at[pl.ds(start + n % CHUNKS * share, share), :]
+        target = (w.gate, w.up)[(n // CHUNKS + d) % 2]
+        piece = target.at[pl.ds((ahead if d else behind) + n % CHUNKS * share, share), :]
         links.arrived(piece, w.gather_s.at[d, n], w.gather_r.at[d, n])
-        return target
-
-    def forward(n):
-        for d, device in enumerate((links.y_up, links.y_down)):
-            target = gathered(d, n)
-            source = pl.ds((ahead if d else behind) + n * share, share)
-            there = pl.ds(opposite + n * share, share)
-            at = 2 * CHUNKS + n
+
+    pieces = hidden_width // PIECE
+    onward = ((links.y_up, w.gate, behind), (links.y_down, w.up, ahead))
+
+    def forward(j):
+        columns = pl.ds(j * PIECE, PIECE)
+        for d, (device, target, start) in enumerate(onward):
             links.start(
-                target.at[source, :], target.at[there, :], w.gather_s.at[d, at], w.gather_r.at[d, at], device
+                target.at[pl.ds(start, depth), columns],
+                target.at[pl.ds(opposite, depth), columns],
+                w.forward_s.at[d, j],
+                w.forward_r.at[d, j],
+                device,
             )
+
+    def forwarded(j):
+        columns = pl.ds(j * PIECE, PIECE)
+        for d, (device, target, start) in enumerate(onward):
+            links.arrived(target.at[pl.ds(opposite, depth), columns], w.forward_s.at[d, j], w.forward_r.at[d, j])
 
     gather(0)
     for load in loads[3:]:
@@ -514,15 +521,16 @@
         carried = jnp.where(links.s >= k + 1, new, carried)
     w.gated[...] = ((w.states[...] + w.decays[...] * carried) * branch).astype(jnp.bfloat16)
 
-    def product(left_ref, right_ref, part_ref, scratch):
+    def product(left_ref, right_ref, part_ref, scratch, total_ref=None):
         tile = 512
         for g in range(GROUPS):
 
             def step(i, carry):
                 columns = pl.ds(aligned(i, tile), tile)
-                part_ref[:, columns] = jnp.dot(
-                    left_ref[...], right_ref[:, columns], preferred_element_type=jnp.float32
-                ).astype(jnp.bfloat16)
+                value = jnp.dot(left_ref[...], right_ref[:, columns], preferred_element_type=jnp.float32)
+                if total_ref is not None:
+                    value = value + total_ref[:, columns]
+                part_ref[:, columns] = value.astype(jnp.bfloat16)
                 return carry
 
             steps = width // (GROUPS * tile)
@@ -554,7 +562,10 @@
     for p in range(4):
         hidden_in[links.xh, pl.ds(own, unit), p * depth : (p + 1) * depth] = w.chosen[:, features(p, links.xh)]
     for n in range(CHUNKS):
-        forward(n)
+        for d in range(2):
+            gathered(d, n)
+    for j in range(pieces):
+        forward(j)
 
     def slot(h, r, side):
         group = links.xh if h == 0 else 1 - links.xh
@@ -573,7 +584,6 @@
         for d in range(2):
             gathered(d, n)
 
-    pieces = hidden_width // PIECE
     top = length // 2
     sides = ((links.x_up, 0), (links.x_down, 1))
 
@@ -595,10 +605,8 @@
         w.lent[j] = partial(1 - links.xh, j, nearby)
     for j in range(pieces):
         w.kept[j] = partial(links.xh, j, nearby)
-    for n in range(CHUNKS):
-        for d in range(2):
-            gathered(d, 2 * CHUNKS + n)
-    for j in range(pieces):
+    def give(j):
+        forwarded(j)
         w.given[j] = (w.lent[j] + partial(1 - links.xh, j, distant)).astype(jnp.bfloat16)
         for device, d in sides:
             links.start(
@@ -608,15 +616,18 @@
                 w.relay_r.at[d, j],
                 device,
             )
-    for j in range(pieces):
+
+    def keep(j):
         w.kept[j] += partial(links.xh, j, distant)
-    for j in range(pieces):
+
+    def pass_on(j):
         for device, d in sides:
             links.arrived(w.relay.at[d, j], w.relay_s.at[d, j], w.relay_r.at[d, j])
             links.start(
                 w.relay.at[d, j], w.taken.at[d, j], w.taken_s.at[d, j], w.taken_r.at[d, j], device
             )
-    for j in range(pieces):
+
+    def take(j):
         for device, d in sides:
             links.arrived(w.taken.at[d, j], w.taken_s.at[d, j], w.taken_r.at[d, j])
             rows = pl.ds(d * top, top)
@@ -625,8 +636,30 @@
                 jax.nn.gelu(both[:, :PIECE], approximate=True) * both[:, PIECE:]
             ).astype(jnp.bfloat16)
 
+    for j in range(pieces):
+        give(j)
+        if j > 0:
+            pass_on(j - 1)
+        keep(j)
+        if j > 2:
+            take(j - 3)
+    pass_on(pieces - 1)
+    take(pieces - 3)
+
     loads[7].wait()
-    product(w.hidden, w.down, w.part2, second)
+    early = (pieces - 2) * PIECE
+
+    def sum_early(i, carry):
+        columns = pl.ds(aligned(i, 512), 512)
+        w.total[:, columns] = jnp.dot(
+            w.hidden[:, :early], w.down[:early, columns], preferred_element_type=jnp.float32
+        )
+        return carry
+
+    lax.fori_loop(0, width // 512, sum_early, 0)
+    take(pieces - 2)
+    take(pieces - 1)
+    product(w.hidden.at[:, pl.ds(early, 2 * PIECE)], w.down.at[pl.ds(early, 2 * PIECE), :], w.part2, second, w.total)
 
     def to_out(columns, total):
         out_ref[pl.ds(own, unit), columns] = (
@@ -702,6 +735,7 @@
         relay=pltpu.VMEM((2, pieces, length // 2, 2 * PIECE), bf),
         taken=pltpu.VMEM((2, pieces, length // 2, 2 * PIECE), bf),
         hidden=pltpu.VMEM((length, hidden_width), bf),
+        total=pltpu.VMEM((length, width), f32),
         part=pltpu.VMEM((length, width), bf),
         part2=pltpu.VMEM((length, width), bf),
         gated=pltpu.VMEM((length, channels), bf),
@@ -714,8 +748,10 @@
         end_s=dma((count - 1,)),
         end_r=dma((count - 1,)),
         load=dma((8,)),
-        gather_s=dma((2, 3 * CHUNKS)),
-        gather_r=dma((2, 3 * CHUNKS)),
+        gather_s=dma((2, 2 * CHUNKS)),
+        gather_r=dma((2, 2 * CHUNKS)),
+        forward_s=dma((2, pieces)),
+        forward_r=dma((2, pieces)),
         far_s=dma((1,)),
         far_r=dma((1,)),
         relay_s=dma((2, pieces)),

time: 116 us -> 113 us (0.974)
  Pallas kernels: 114 us -> 112 us
    pallas_call x1, Pallas kernels: 114 us -> 112 us  [on_device(): pl.pallas_call(functools.partial(layer_kernel, count, conv_weight.shape[0...]
where the time goes in v3:
time: 113 us
  Pallas kernels  112 us (99%)
  local copies, waits for them, and re-layouts  1.32 us (1%)
    pallas_call x1, Pallas kernels, on_device(): pl.pallas_call(functools.partial(layer_kernel, count, conv_weight.shape[0...  112 us

profile of v3, /device:TPU:1, one launch (start us, length us, event | category | flops | bytes accessed | tf_op | source)
XLA Modules:
  0.0 113.2 jit_solution(12506285356447368842)
XLA Ops:
  0.0 111.9 %shard_map.154 = bf16[256,4096]{1,0:T(8,128)(2,1)S(1)} custom-call(f32[1,4096]{1,0:T(1,128)} %bitcast.6, f32[4,256]{1,0:T(4,128)} %refs_1_.1, f32[1,256]{1,0:T(1,128)} %bitcast.8, bf16[1,256,256]{2,1,0:T(8,128)(2,1)} %refs_3_.1, f32[1,256]{1,0:T(1,128)} %bitcast.9, bf16[1,256,256]{2,1,0:T(8,128)(2,1)} %refs_5_.1, f32[1,256]{1,0:T(1,128)} %bitcast.10, ...), custom_call_target="tpu_custom_call" | custom-call | tf_op jit(solution)/shard_map/pallas_call | solution.py:762
  111.9 1.3 %copy.18 = bf16[256,4096]{1,0:T(8,128)(2,1)} copy(bf16[256,4096]{1,0:T(8,128)(2,1)S(1)} %shard_map.154) | data formatting | bytes 4194304

commit v4 on v3

--- a/solution.py
+++ b/solution.py
@@ -136,20 +136,20 @@
         self.near = (8 * (1 - self.xl) + 2 * z + core, s)
         self.far = (t, 2 * y + 1 - self.xh)
         self.outside = (8 * (1 - self.xl) + 2 * z + core, lax.select(self.xl == 0, self.x_down[1], self.x_up[1]))
-        self.sent = []
+        self.all_sent = []
 
     def start(self, source, target, send, recv, device):
-        copy = remote(source, target, send, recv, *device)
-        copy.start()
-        self.sent.append(copy)
-
-    def arrived(self, target, send, recv):
-        remote(target, target, send, recv, *self.pair).wait_recv()
+        remote(source, target, send, recv, *device).start()
+
+    def arrived(self, target, recv):
+        remote(target, target, recv, recv, *self.pair).wait_recv()
+
+    def sent_in_all(self, like, send):
+        self.all_sent.append(remote(like, like, send, send, *self.pair))
 
     def drain(self):
-        for copy in self.sent:
-            copy.wait_send()
-        self.sent = []
+        for copies in self.all_sent:
+            copies.wait_send()
 
 
 GROUPS = 2
@@ -172,17 +172,15 @@
         out_near=pltpu.VMEM((unit, width), bf),
         from_near=pltpu.VMEM((GROUPS, unit, 2 * quarter), bf),
         own=pltpu.VMEM((unit, width), jnp.float32),
-        pair_s=dma((4, GROUPS)),
+        pair_s=dma,
         pair_r=dma((4, GROUPS)),
-        far_up_s=dma((GROUPS,)),
         far_up_r=dma((GROUPS,)),
-        far_down_s=dma((GROUPS,)),
         far_down_r=dma((GROUPS,)),
-        up_s=dma((2 * GROUPS,)),
+        up_s=dma,
         up_r=dma((2 * GROUPS,)),
-        down_s=dma((2 * GROUPS,)),
+        down_s=dma,
         down_r=dma((2 * GROUPS,)),
-        near_s=dma((GROUPS,)),
+        near_s=dma,
         near_r=dma((GROUPS,)),
     )
 
@@ -200,7 +198,7 @@
         links.start(
             part.at[pl.ds(aligned(block, rows), rows), columns],
             b.pair.at[k, :, columns],
-            b.pair_s.at[k, g],
+            b.pair_s,
             b.pair_r.at[k, g],
             links.pair,
         )
@@ -220,30 +218,30 @@
 
     def paired(k, g):
         columns = pl.ds(g * 2 * quarter, 2 * quarter)
-        links.arrived(b.pair.at[k, :, columns], b.pair_s.at[k, g], b.pair_r.at[k, g])
+        links.arrived(b.pair.at[k, :, columns], b.pair_r.at[k, g])
 
     def send_far(g):
         paired(0, g)
         for q, landing, send, recv, device in (
-            (2 * g, b.far_up, b.far_up_s, b.far_up_r, links.z_up),
-            (2 * g + 1, b.far_down, b.far_down_s, b.far_down_r, links.z_down),
+            (2 * g, b.far_up, b.up_s, b.far_up_r, links.z_up),
+            (2 * g + 1, b.far_down, b.down_s, b.far_down_r, links.z_down),
         ):
             columns = pl.ds(q * quarter, quarter)
             b.out_far[:, columns] = summed(0, q).astype(jnp.bfloat16)
-            links.start(b.out_far.at[:, columns], landing.at[g], send.at[g], recv.at[g], device)
+            links.start(b.out_far.at[:, columns], landing.at[g], send, recv.at[g], device)
 
     def send_up(q, value):
         columns = pl.ds(q * quarter, quarter)
         b.out_up[:, columns] = value.astype(jnp.bfloat16)
         links.start(
-            b.out_up.at[:, columns], b.from_down.at[q], b.up_s.at[q], b.up_r.at[q], links.z_up
+            b.out_up.at[:, columns], b.from_down.at[q], b.up_s, b.up_r.at[q], links.z_up
         )
 
     def send_down(q, value):
         columns = pl.ds(q * quarter, quarter)
         b.out_down[:, columns] = value.astype(jnp.bfloat16)
         links.start(
-            b.out_down.at[:, columns], b.from_up.at[q], b.down_s.at[q], b.down_r.at[q], links.z_down
+            b.out_down.at[:, columns], b.from_up.at[q], b.down_s, b.down_r.at[q], links.z_down
         )
 
     def send_first(g):
@@ -253,16 +251,16 @@
         send_down(2 * g, summed(2, 2 * g))
 
     def send_second(g):
-        links.arrived(b.far_up.at[g], b.far_up_s.at[g], b.far_up_r.at[g])
+        links.arrived(b.far_up.at[g], b.far_up_r.at[g])
         send_up(2 * g, summed(1, 2 * g) + b.far_up[g].astype(jnp.float32))
-        links.arrived(b.far_down.at[g], b.far_down_s.at[g], b.far_down_r.at[g])
+        links.arrived(b.far_down.at[g], b.far_down_r.at[g])
         send_down(2 * g + 1, summed(2, 2 * g + 1) + b.far_down[g].astype(jnp.float32))
 
     def collect(g):
         paired(3, g)
         for q in (2 * g, 2 * g + 1):
-            links.arrived(b.from_down.at[q], b.up_s.at[q], b.up_r.at[q])
-            links.arrived(b.from_up.at[q], b.down_s.at[q], b.down_r.at[q])
+            links.arrived(b.from_down.at[q], b.up_r.at[q])
+            links.arrived(b.from_up.at[q], b.down_r.at[q])
             columns = pl.ds(q * quarter, quarter)
             total = (
                 summed(3, q)
@@ -277,7 +275,7 @@
         links.start(
             b.out_near.at[:, columns],
             b.from_near.at[g],
-            b.near_s.at[g],
+            b.near_s,
             b.near_r.at[g],
             links.near,
         )
@@ -293,82 +291,77 @@
     for g in range(GROUPS):
         collect(g)
     for g in range(GROUPS):
-        links.arrived(b.from_near.at[g], b.near_s.at[g], b.near_r.at[g])
+        links.arrived(b.from_near.at[g], b.near_r.at[g])
         columns = pl.ds(g * 2 * quarter, 2 * quarter)
         finish(columns, b.own[:, columns] + b.from_near[g].astype(jnp.float32))
 
-
-def gather_scratch():
+    links.sent_in_all(part.at[pl.ds(0, 4 * rows), :], b.pair_s)
+    links.sent_in_all(part.at[pl.ds(0, 3 * unit), :], b.up_s)
+    links.sent_in_all(part.at[pl.ds(0, 3 * unit), :], b.down_s)
+    links.sent_in_all(part.at[pl.ds(0, unit), :], b.near_s)
+
+
+def gather_scratch(pairs):
     dma = pltpu.SemaphoreType.DMA
     return dict(
-        near_s=dma((2,)),
+        near_s=dma,
         near_r=dma((2,)),
-        up_s=dma((2, 2)),
+        up_s=dma,
         up_r=dma((2, 2)),
-        down_s=dma((2, 2)),
+        down_s=dma,
         down_r=dma((2, 2)),
-        far_up_s=dma((2, 2)),
         far_up_r=dma((2, 2)),
-        far_down_s=dma((2, 2)),
         far_down_r=dma((2, 2)),
-        pair_s=dma((2, 10)),
-        pair_r=dma((2, 10)),
-    )
-
-
-def all_gather(links, slot, unit, b, ready):
-    core, z, xl = links.core, links.z, links.xl
-
-    def row(step, i, c=core):
-        across = xl if i == 0 else 1 - xl
-        return owned_row(links, c, lax.rem(z + step, 4), across, unit)
-
-    def pass_on(h, n, r, half):
-        piece = slot(h, r, half)
-        links.start(piece, piece, b.pair_s.at[h, n], b.pair_r.at[h, n], links.pair)
-
-    def send(h, i, r):
-        piece = slot(h, r, None)
-        links.start(piece, piece, b.up_s.at[h, i], b.up_r.at[h, i], links.z_up)
-        links.start(piece, piece, b.down_s.at[h, i], b.down_r.at[h, i], links.z_down)
-
-    for h in range(2):
-        ready(h)
-        own = row(0, 0)
-        piece = slot(h, own, None)
-        links.start(piece, piece, b.near_s.at[h], b.near_r.at[h], links.near)
-        send(h, 0, own)
-        pass_on(h, 0, own, None)
-    for h in range(2):
-        r = row(0, 1)
-        links.arrived(slot(h, r, None), b.near_s.at[h], b.near_r.at[h])
-        send(h, 1, r)
-        pass_on(h, 1, r, None)
-    for i in range(2):
-        for h in range(2):
-            r = row(3, i)
-            links.arrived(slot(h, r, None), b.up_s.at[h, i], b.up_r.at[h, i])
-            piece = slot(h, r, 0)
-            links.start(piece, piece, b.far_up_s.at[h, i], b.far_up_r.at[h, i], links.z_up)
-            pass_on(h, 2 + i, r, None)
-            r = row(1, i)
-            links.arrived(slot(h, r, None), b.down_s.at[h, i], b.down_r.at[h, i])
-            piece = slot(h, r, 1)
-            links.start(piece, piece, b.far_down_s.at[h, i], b.far_down_r.at[h, i], links.z_down)
-            pass_on(h, 4 + i, r, None)
-    for i in range(2):
-        for h in range(2):
-            r = row(2, i)
-            links.arrived(slot(h, r, 0), b.far_up_s.at[h, i], b.far_up_r.at[h, i])
-            pass_on(h, 6 + i, r, 0)
-            links.arrived(slot(h, r, 1), b.far_down_s.at[h, i], b.far_down_r.at[h, i])
-            pass_on(h, 8 + i, r, 1)
-    for n, (step, i, half) in enumerate(
-        [(0, 0, None), (0, 1, None), (3, 0, None), (3, 1, None), (1, 0, None), (1, 1, None)]
-        + [(2, 0, 0), (2, 1, 0), (2, 0, 1), (2, 1, 1)]
-    ):
-        for h in range(2):
-            links.arrived(slot(h, row(step, i, 1 - core), half), b.pair_s.at[h, n], b.pair_r.at[h, n])
+        pair_s=dma,
+        pair_r=dma((pairs,)),
+    )
+
+
+class Gather:
+    def __init__(self, links, slot, unit, b, pair_of):
+        self.links, self.slot, self.unit, self.b, self.pair_of = links, slot, unit, b, pair_of
+
+    def row(self, step, i):
+        links = self.links
+        across = links.xl if i == 0 else 1 - links.xl
+        return owned_row(links, links.core, lax.rem(links.z + step, 4), across, self.unit)
+
+    def pass_on(self, h, r, half=None):
+        piece = self.slot(h, r, half)
+        self.links.start(piece, piece, self.b.pair_s, self.b.pair_r.at[self.pair_of[h]], self.links.pair)
+
+    def near(self, h):
+        piece = self.slot(h, self.row(0, 0), None)
+        self.links.start(piece, piece, self.b.near_s, self.b.near_r.at[h], self.links.near)
+
+    def send(self, h, i):
+        links, b = self.links, self.b
+        piece = self.slot(h, self.row(0, i), None)
+        links.start(piece, piece, b.up_s, b.up_r.at[h, i], links.z_up)
+        links.start(piece, piece, b.down_s, b.down_r.at[h, i], links.z_down)
+        self.pass_on(h, self.row(0, i))
+
+    def from_near(self, h):
+        self.links.arrived(self.slot(h, self.row(0, 1), None), self.b.near_r.at[h])
+        self.send(h, 1)
+
+    def relay(self, h, i):
+        links, b = self.links, self.b
+        for step, side, recv, send, far, device in (
+            (3, 0, b.up_r, b.up_s, b.far_up_r, links.z_up),
+            (1, 1, b.down_r, b.down_s, b.far_down_r, links.z_down),
+        ):
+            r = self.row(step, i)
+            links.arrived(self.slot(h, r, None), recv.at[h, i])
+            piece = self.slot(h, r, side)
+            links.start(piece, piece, send, far.at[h, i], device)
+            self.pass_on(h, r)
+
+    def relayed(self, h, i):
+        r = self.row(2, i)
+        for side, recv in ((0, self.b.far_up_r), (1, self.b.far_down_r)):
+            self.links.arrived(self.slot(h, r, side), recv.at[h, i])
+            self.pass_on(h, r, side)
 
 
 PIECE = 128
@@ -440,13 +433,13 @@
             source, target = sides[(n // CHUNKS + d) % 2]
             there = pl.ds((ahead if d else behind) + n % CHUNKS * share, share)
             links.start(
-                source.at[rows, :], target.at[there, :], w.gather_s.at[d, n], w.gather_r.at[d, n], device
+                source.at[rows, :], target.at[there, :], w.gather_s, w.gather_r.at[d, n // CHUNKS], device
             )
 
-    def gathered(d, n):
-        target = (w.gate, w.up)[(n // CHUNKS + d) % 2]
-        piece = target.at[pl.ds((ahead if d else behind) + n % CHUNKS * share, share), :]
-        links.arrived(piece, w.gather_s.at[d, n], w.gather_r.at[d, n])
+    def gathered(n):
+        for d in range(2):
+            target = (w.gate, w.up)[(n + d) % 2]
+            links.arrived(target.at[pl.ds(ahead if d else behind, depth), :], w.gather_r.at[d, n])
 
     pieces = hidden_width // PIECE
     onward = ((links.y_up, w.gate, behind), (links.y_down, w.up, ahead))
@@ -457,7 +450,7 @@
             links.start(
                 target.at[pl.ds(start, depth), columns],
                 target.at[pl.ds(opposite, depth), columns],
-                w.forward_s.at[d, j],
+                w.forward_s,
                 w.forward_r.at[d, j],
                 device,
             )
@@ -465,7 +458,7 @@
     def forwarded(j):
         columns = pl.ds(j * PIECE, PIECE)
         for d, (device, target, start) in enumerate(onward):
-            links.arrived(target.at[pl.ds(opposite, depth), columns], w.forward_s.at[d, j], w.forward_r.at[d, j])
+            links.arrived(target.at[pl.ds(opposite, depth), columns], w.forward_r.at[d, j])
 
     gather(0)
     for load in loads[3:]:
@@ -485,7 +478,7 @@
         load.wait()
     loads[0].wait()
     lax.fori_loop(0, 16, norm_step, 0)
-    links.arrived(w.normed.at[edge, :], w.tail_s, w.tail_r)
+    links.arrived(w.normed.at[edge, :], w.tail_r)
     norm(length, EDGE)
     loads[1].wait()
     w.inner[...] = jnp.dot(w.normed[...], w.in_proj[...], preferred_element_type=jnp.float32).astype(
@@ -507,7 +500,7 @@
         w.ends,
     )
     for k in range(count - 1):
-        links.start(w.ends, w.arrived.at[k], w.end_s.at[k], w.end_r.at[k], peers[k])
+        links.start(w.ends, w.arrived.at[k], w.end_s, w.end_r, peers[k])
     for n in range(1, 2 * CHUNKS):
         gather(n)
     loads[2].wait()
@@ -515,8 +508,8 @@
         jnp.dot(w.normed[:length, :], w.branch_proj[...], preferred_element_type=jnp.float32), approximate=True
     )
     carried = jnp.zeros((1, w.ends.shape[1]), jnp.float32)
+    links.arrived(w.arrived, w.end_r)
     for k in range(count - 2, -1, -1):
-        links.arrived(w.arrived.at[k], w.end_s.at[k], w.end_r.at[k])
         new = w.arrived[k, 0:1, :] * carried + w.arrived[k, 1:2, :]
         carried = jnp.where(links.s >= k + 1, new, carried)
     w.gated[...] = ((w.states[...] + w.decays[...] * carried) * branch).astype(jnp.bfloat16)
@@ -554,35 +547,39 @@
     def features(p, which):
         return pl.ds(aligned(2 * lax.rem(links.y + 3 + p, 4) + which, depth), depth)
 
-    for p in range(4):
-        w.away[:, p * depth : (p + 1) * depth] = w.chosen[:, features(p, 1 - links.xh)]
-    links.start(
-        w.away, hidden_in.at[links.xh, pl.ds(own, unit), :], w.far_s.at[0], w.far_r.at[0], links.far
-    )
-    for p in range(4):
-        hidden_in[links.xh, pl.ds(own, unit), p * depth : (p + 1) * depth] = w.chosen[:, features(p, links.xh)]
-    for n in range(CHUNKS):
-        for d in range(2):
-            gathered(d, n)
-    for j in range(pieces):
-        forward(j)
-
     def slot(h, r, side):
         group = links.xh if h == 0 else 1 - links.xh
         columns = pl.ds(0, half) if side is None else pl.ds(side * (half // 2), half // 2)
         return hidden_in.at[group, pl.ds(r, unit), columns]
 
-    def ready(h):
-        if h == 1:
-            links.arrived(slot(1, own, None), w.far_s.at[0], w.far_r.at[0])
-
-    all_gather(links, slot, unit, spread, ready)
+    tokens = Gather(links, slot, unit, spread, (0, 1))
+    for p in range(4):
+        w.away[:, p * depth : (p + 1) * depth] = w.chosen[:, features(p, 1 - links.xh)]
+    landing = hidden_in.at[links.xh, pl.ds(own, unit), :]
+    links.start(w.away, landing, w.far_s, w.far_r.at[0], links.far)
+    links.start(w.away, landing, w.far_s, w.far_r.at[1], links.outside)
+    for p in range(4):
+        hidden_in[links.xh, pl.ds(own, unit), p * depth : (p + 1) * depth] = w.chosen[:, features(p, links.xh)]
+    tokens.near(0)
+    tokens.send(0, 0)
+    gathered(0)
+    for j in range(pieces):
+        forward(j)
+    for i in (1, 0):
+        links.arrived(slot(1, tokens.row(0, i), None), w.far_r.at[i])
+        tokens.send(1, i)
+    for i in (1, 0):
+        tokens.relay(1, i)
+    tokens.relay(0, 0)
+    tokens.from_near(0)
+    for i in (1, 0):
+        tokens.relayed(1, i)
+    others = pl.ds(aligned(1 - links.core, length // 2), length // 2)
+    links.arrived(hidden_in.at[1 - links.xh, others, :], spread.pair_r.at[1])
 
     loads[5].wait()
     loads[6].wait()
-    for n in range(CHUNKS, 2 * CHUNKS):
-        for d in range(2):
-            gathered(d, n)
+    gathered(1)
 
     top = length // 2
     sides = ((links.x_up, 0), (links.x_down, 1))
@@ -603,8 +600,7 @@
     nearby, distant = pl.ds(0, opposite), pl.ds(opposite, depth)
     for j in range(pieces):
         w.lent[j] = partial(1 - links.xh, j, nearby)
-    for j in range(pieces):
-        w.kept[j] = partial(links.xh, j, nearby)
+
     def give(j):
         forwarded(j)
         w.given[j] = (w.lent[j] + partial(1 - links.xh, j, distant)).astype(jnp.bfloat16)
@@ -612,39 +608,43 @@
             links.start(
                 w.given.at[j, pl.ds(d * top, top), :],
                 w.relay.at[d, j],
-                w.relay_s.at[d, j],
+                w.relay_s,
                 w.relay_r.at[d, j],
                 device,
             )
 
     def keep(j):
-        w.kept[j] += partial(links.xh, j, distant)
+        w.kept[j] = partial(links.xh, j, pl.ds(0, 4 * depth))
 
     def pass_on(j):
         for device, d in sides:
-            links.arrived(w.relay.at[d, j], w.relay_s.at[d, j], w.relay_r.at[d, j])
+            links.arrived(w.relay.at[d, j], w.relay_r.at[d, j])
             links.start(
-                w.relay.at[d, j], w.taken.at[d, j], w.taken_s.at[d, j], w.taken_r.at[d, j], device
+                w.relay.at[d, j], w.taken.at[d, j], w.taken_s, w.taken_r.at[d, j], device
             )
 
     def take(j):
         for device, d in sides:
-            links.arrived(w.taken.at[d, j], w.taken_s.at[d, j], w.taken_r.at[d, j])
+            links.arrived(w.taken.at[d, j], w.taken_r.at[d, j])
             rows = pl.ds(d * top, top)
             both = w.kept[j, rows, :] + w.taken[d, j].astype(jnp.float32)
             w.hidden[rows, j * PIECE : (j + 1) * PIECE] = (
                 jax.nn.gelu(both[:, :PIECE], approximate=True) * both[:, PIECE:]
             ).astype(jnp.bfloat16)
 
+    give(0)
+    tokens.relay(0, 1)
+    for i in range(2):
+        tokens.relayed(0, i)
+    links.arrived(hidden_in.at[links.xh, others, :], spread.pair_r.at[0])
+    give(1)
     for j in range(pieces):
-        give(j)
-        if j > 0:
-            pass_on(j - 1)
+        pass_on(j)
+        if j + 2 < pieces:
+            give(j + 2)
         keep(j)
-        if j > 2:
-            take(j - 3)
-    pass_on(pieces - 1)
-    take(pieces - 3)
+        if j > 1:
+            take(j - 2)
 
     loads[7].wait()
     early = (pieces - 2) * PIECE
@@ -672,7 +672,33 @@
         size = half if side is None else half // 2
         return out_ref.at[pl.ds(r, unit), pl.ds(h * half + (0 if side is None else side * size), size)]
 
-    all_gather(links, place, unit, final, lambda h: None)
+    rows = Gather(links, place, unit, final, (0, 0))
+    for h in range(2):
+        rows.near(h)
+        rows.send(h, 0)
+    for h in range(2):
+        rows.from_near(h)
+    for i in range(2):
+        for h in range(2):
+            rows.relay(h, i)
+    for i in range(2):
+        for h in range(2):
+            rows.relayed(h, i)
+    links.arrived(out_ref.at[others, :], final.pair_r.at[0])
+
+    links.sent_in_all(w.normed.at[edge, :], w.tail_s)
+    links.sent_in_all(w.arrived, w.end_s)
+    links.sent_in_all(w.gate, w.gather_s)
+    links.sent_in_all(w.gate.at[pl.ds(0, 2 * depth), :], w.forward_s)
+    links.sent_in_all(w.chosen, w.far_s)
+    links.sent_in_all(w.given, w.relay_s)
+    links.sent_in_all(w.relay, w.taken_s)
+    links.sent_in_all(w.away, spread.near_s)
+    links.sent_in_all(w.chosen, final.near_s)
+    for b in (spread, final):
+        links.sent_in_all(out_ref.at[pl.ds(0, 3 * unit), :], b.up_s)
+        links.sent_in_all(out_ref.at[pl.ds(0, 3 * unit), :], b.down_s)
+        links.sent_in_all(out_ref.at[others, :], b.pair_s)
     links.drain()
 
 
@@ -745,18 +771,18 @@
         arrived=pltpu.VMEM((count - 1, 8, channels), f32),
         tail_s=dma,
         tail_r=dma,
-        end_s=dma((count - 1,)),
-        end_r=dma((count - 1,)),
+        end_s=dma,
+        end_r=dma,
         load=dma((8,)),
-        gather_s=dma((2, 2 * CHUNKS)),
-        gather_r=dma((2, 2 * CHUNKS)),
-        forward_s=dma((2, pieces)),
+        gather_s=dma,
+        gather_r=dma((2, 2)),
+        forward_s=dma,
         forward_r=dma((2, pieces)),
-        far_s=dma((1,)),
-        far_r=dma((1,)),
-        relay_s=dma((2, pieces)),
+        far_s=dma,
+        far_r=dma((2,)),
+        relay_s=dma,
         relay_r=dma((2, pieces)),
-        taken_s=dma((2, pieces)),
+        taken_s=dma,
         taken_r=dma((2, pieces)),
     )
     return pl.pallas_call(
@@ -768,8 +794,8 @@
             scratch,
             scatter_scratch(length, width),
             scatter_scratch(length, width),
-            gather_scratch(),
-            gather_scratch(),
+            gather_scratch(2),
+            gather_scratch(1),
         ),
         compiler_params=pltpu.CompilerParams(
             collective_id=0, has_side_effects=True, vmem_limit_bytes=GRANT

time: 113 us -> 109 us (0.965)
  Pallas kernels: 112 us -> 107 us
    pallas_call x1, Pallas kernels: 112 us -> 107 us  [on_device(): pl.pallas_call(functools.partial(layer_kernel, count, conv_weight.shape[0...]
where the time goes in v4:
time: 109 us; the launch traced here: 108 us
  Pallas kernels  107 us (98%)
  local copies, waits for them, and re-layouts  1.32 us (1%)
    pallas_call x1, Pallas kernels, on_device(): pl.pallas_call(functools.partial(layer_kernel, count, conv_weight.shape[0...  107 us

profile of v4, /device:TPU:1, one launch (start us, length us, event | category | flops | bytes accessed | tf_op | source)
XLA Modules:
  0.0 108.5 jit_solution(6511641544895601864)
XLA Ops:
  0.0 107.1 %shard_map.154 = bf16[256,4096]{1,0:T(8,128)(2,1)S(1)} custom-call(f32[1,4096]{1,0:T(1,128)} %bitcast.6, f32[4,256]{1,0:T(4,128)} %refs_1_.1, f32[1,256]{1,0:T(1,128)} %bitcast.8, bf16[1,256,256]{2,1,0:T(8,128)(2,1)} %refs_3_.1, f32[1,256]{1,0:T(1,128)} %bitcast.9, bf16[1,256,256]{2,1,0:T(8,128)(2,1)} %refs_5_.1, f32[1,256]{1,0:T(1,128)} %bitcast.10, ...), custom_call_target="tpu_custom_call" | custom-call | tf_op jit(solution)/shard_map/pallas_call | solution.py:788
  107.1 1.3 %copy.18 = bf16[256,4096]{1,0:T(8,128)(2,1)} copy(bf16[256,4096]{1,0:T(8,128)(2,1)S(1)} %shard_map.154) | data formatting | bytes 4194304

commit v5 on v4

--- a/solution.py
+++ b/solution.py
@@ -179,7 +179,6 @@
         up_s=dma,
         up_r=dma((2 * GROUPS,)),
         down_s=dma,
-        down_r=dma((2 * GROUPS,)),
         near_s=dma,
         near_r=dma((GROUPS,)),
     )
@@ -241,7 +240,7 @@
         columns = pl.ds(q * quarter, quarter)
         b.out_down[:, columns] = value.astype(jnp.bfloat16)
         links.start(
-            b.out_down.at[:, columns], b.from_up.at[q], b.down_s, b.down_r.at[q], links.z_down
+            b.out_down.at[:, columns], b.from_up.at[q], b.down_s, b.up_r.at[q], links.z_down
         )
 
     def send_first(g):
@@ -259,8 +258,7 @@
     def collect(g):
         paired(3, g)
         for q in (2 * g, 2 * g + 1):
-            links.arrived(b.from_down.at[q], b.up_r.at[q])
-            links.arrived(b.from_up.at[q], b.down_r.at[q])
+            links.arrived(b.from_down.at[pl.ds(0, 2)], b.up_r.at[q])
             columns = pl.ds(q * quarter, quarter)
             total = (
                 summed(3, q)
@@ -446,21 +444,19 @@
 
     def forward(j):
         columns = pl.ds(j * PIECE, PIECE)
-        for d, (device, target, start) in enumerate(onward):
+        for device, target, start in onward:
             links.start(
                 target.at[pl.ds(start, depth), columns],
                 target.at[pl.ds(opposite, depth), columns],
                 w.forward_s,
-                w.forward_r.at[d, j],
+                w.forward_r.at[j],
                 device,
             )
 
     def forwarded(j):
         columns = pl.ds(j * PIECE, PIECE)
-        for d, (device, target, start) in enumerate(onward):
-            links.arrived(target.at[pl.ds(opposite, depth), columns], w.forward_r.at[d, j])
-
-    gather(0)
+        links.arrived(w.gate.at[pl.ds(ahead, 2 * depth), columns], w.forward_r.at[j])
+
     for load in loads[3:]:
         load.start()
 
@@ -477,8 +473,9 @@
     for load in small_loads:
         load.wait()
     loads[0].wait()
-    lax.fori_loop(0, 16, norm_step, 0)
+    lax.fori_loop(0, 16, norm_step, 0, unroll=4)
     links.arrived(w.normed.at[edge, :], w.tail_r)
+    gather(0)
     norm(length, EDGE)
     loads[1].wait()
     w.inner[...] = jnp.dot(w.normed[...], w.in_proj[...], preferred_element_type=jnp.float32).astype(
@@ -527,7 +524,7 @@
                 return carry
 
             steps = width // (GROUPS * tile)
-            lax.fori_loop(g * steps, (g + 1) * steps, step, 0)
+            lax.fori_loop(g * steps, (g + 1) * steps, step, 0, unroll=True)
             pair_up(links, part_ref, scratch, g)
 
     loads[3].wait()
@@ -584,12 +581,12 @@
     top = length // 2
     sides = ((links.x_up, 0), (links.x_down, 1))
 
-    def partial(group, j, place):
+    def partial(group, j):
         return jnp.concatenate(
             [
                 jnp.dot(
-                    hidden_in[group, :, place],
-                    weights[place, j * PIECE : (j + 1) * PIECE],
+                    hidden_in[group],
+                    weights[:, j * PIECE : (j + 1) * PIECE],
                     preferred_element_type=jnp.float32,
                 )
                 for weights in (w.gate, w.up)
@@ -597,35 +594,31 @@
             axis=1,
         )
 
-    nearby, distant = pl.ds(0, opposite), pl.ds(opposite, depth)
-    for j in range(pieces):
-        w.lent[j] = partial(1 - links.xh, j, nearby)
-
     def give(j):
         forwarded(j)
-        w.given[j] = (w.lent[j] + partial(1 - links.xh, j, distant)).astype(jnp.bfloat16)
+        w.given[j] = partial(1 - links.xh, j).astype(jnp.bfloat16)
         for device, d in sides:
             links.start(
                 w.given.at[j, pl.ds(d * top, top), :],
                 w.relay.at[d, j],
                 w.relay_s,
-                w.relay_r.at[d, j],
+                w.relay_r.at[j],
                 device,
             )
 
     def keep(j):
-        w.kept[j] = partial(links.xh, j, pl.ds(0, 4 * depth))
+        w.kept[j] = partial(links.xh, j)
 
     def pass_on(j):
+        links.arrived(w.relay.at[:, j], w.relay_r.at[j])
         for device, d in sides:
-            links.arrived(w.relay.at[d, j], w.relay_r.at[d, j])
             links.start(
-                w.relay.at[d, j], w.taken.at[d, j], w.taken_s, w.taken_r.at[d, j], device
+                w.relay.at[d, j], w.taken.at[d, j], w.taken_s, w.taken_r.at[j], device
             )
 
     def take(j):
+        links.arrived(w.taken.at[:, j], w.taken_r.at[j])
         for device, d in sides:
-            links.arrived(w.taken.at[d, j], w.taken_r.at[d, j])
             rows = pl.ds(d * top, top)
             both = w.kept[j, rows, :] + w.taken[d, j].astype(jnp.float32)
             w.hidden[rows, j * PIECE : (j + 1) * PIECE] = (
@@ -633,15 +626,16 @@
             ).astype(jnp.bfloat16)
 
     give(0)
+    give(1)
     tokens.relay(0, 1)
-    for i in range(2):
-        tokens.relayed(0, i)
-    links.arrived(hidden_in.at[links.xh, others, :], spread.pair_r.at[0])
-    give(1)
     for j in range(pieces):
         pass_on(j)
         if j + 2 < pieces:
             give(j + 2)
+        if j == 0:
+            for i in range(2):
+                tokens.relayed(0, i)
+            links.arrived(hidden_in.at[links.xh, others, :], spread.pair_r.at[0])
         keep(j)
         if j > 1:
             take(j - 2)
@@ -656,7 +650,7 @@
         )
         return carry
 
-    lax.fori_loop(0, width // 512, sum_early, 0)
+    lax.fori_loop(0, width // 512, sum_early, 0, unroll=4)
     take(pieces - 2)
     take(pieces - 1)
     product(w.hidden.at[:, pl.ds(early, 2 * PIECE)], w.down.at[pl.ds(early, 2 * PIECE), :], w.part2, second, w.total)
@@ -756,7 +750,6 @@
         down=pltpu.VMEM(down_proj.shape, bf),
         hidden_in=pltpu.VMEM((2, length, width // 2), bf),
         given=pltpu.VMEM((pieces, length, 2 * PIECE), bf),
-        lent=pltpu.VMEM((pieces, length, 2 * PIECE), f32),
         kept=pltpu.VMEM((pieces, length, 2 * PIECE), f32),
         relay=pltpu.VMEM((2, pieces, length // 2, 2 * PIECE), bf),
         taken=pltpu.VMEM((2, pieces, length // 2, 2 * PIECE), bf),
@@ -777,13 +770,13 @@
         gather_s=dma,
         gather_r=dma((2, 2)),
         forward_s=dma,
-        forward_r=dma((2, pieces)),
+        forward_r=dma((pieces,)),
         far_s=dma,
         far_r=dma((2,)),
         relay_s=dma,
-        relay_r=dma((2, pieces)),
+        relay_r=dma((pieces,)),
         taken_s=dma,
-        taken_r=dma((2, pieces)),
+        taken_r=dma((pieces,)),
     )
     return pl.pallas_call(
         functools.partial(layer_kernel, count, conv_weight.shape[0]),

time: 109 us -> 108 us (level)
  no operation moved by 1% of the time
where the time goes in v5:
time: 108 us
  Pallas kernels  106 us (98%)
  local copies, waits for them, and re-layouts  1.32 us (1%)
    pallas_call x1, Pallas kernels, on_device(): pl.pallas_call(functools.partial(layer_kernel, count, conv_weight.shape[0...  106 us

profile of v5, /device:TPU:1, one launch (start us, length us, event | category | flops | bytes accessed | tf_op | source)
XLA Modules:
  0.0 107.7 jit_solution(4979236136715306046)
XLA Ops:
  0.0 106.4 %shard_map.154 = bf16[256,4096]{1,0:T(8,128)(2,1)S(1)} custom-call(f32[1,4096]{1,0:T(1,128)} %bitcast.6, f32[4,256]{1,0:T(4,128)} %refs_1_.1, f32[1,256]{1,0:T(1,128)} %bitcast.8, bf16[1,256,256]{2,1,0:T(8,128)(2,1)} %refs_3_.1, f32[1,256]{1,0:T(1,128)} %bitcast.9, bf16[1,256,256]{2,1,0:T(8,128)(2,1)} %refs_5_.1, f32[1,256]{1,0:T(1,128)} %bitcast.10, ...), custom_call_target="tpu_custom_call" | custom-call | tf_op jit(solution)/shard_map/pallas_call | solution.py:781
  106.4 1.3 %copy.18 = bf16[256,4096]{1,0:T(8,128)(2,1)} copy(bf16[256,4096]{1,0:T(8,128)(2,1)S(1)} %shard_map.154) | data formatting | bytes 4194304

commit v6 on v5

--- a/solution.py
+++ b/solution.py
@@ -365,7 +365,8 @@
 PIECE = 128
 
 
-CHUNKS = 4
+CHUNKS = 8
+PARTS = 4
 
 
 def layer_kernel(
@@ -390,7 +391,7 @@
 
     behind, here, ahead, opposite = (p * depth for p in range(4))
     loads = [
-        pltpu.make_async_copy(residual_ref, w.normed.at[pl.ds(0, length), :], w.load.at[0]),
+        pltpu.make_async_copy(residual_ref.at[pl.ds(length - EDGE, EDGE), :], w.edge, w.load.at[0]),
         pltpu.make_async_copy(in_proj_ref, w.in_proj, w.load.at[1]),
         pltpu.make_async_copy(branch_proj_ref, w.branch_proj, w.load.at[2]),
         pltpu.make_async_copy(out_proj_ref, w.out_proj, w.load.at[3]),
@@ -399,11 +400,20 @@
         pltpu.make_async_copy(up_proj_ref, w.up.at[pl.ds(here, depth), :], w.load.at[6]),
         pltpu.make_async_copy(down_proj_ref, w.down, w.load.at[7]),
     ]
+    part_rows = length // PARTS
+    row_loads = [
+        pltpu.make_async_copy(
+            residual_ref.at[pl.ds(k * part_rows, part_rows), :],
+            w.normed.at[pl.ds(k * part_rows, part_rows), :],
+            w.row_load.at[k],
+        )
+        for k in range(PARTS)
+    ]
     small_loads = [
         pltpu.make_async_copy(source, target, w.small_load.at[k])
         for k, (source, target) in enumerate(zip(outside, w.small))
     ]
-    for load in loads[:2] + small_loads + loads[2:3]:
+    for load in loads[:1] + small_loads[:1] + row_loads + loads[1:2] + small_loads[1:] + loads[2:3]:
         load.start()
     (
         mix_gain_ref,
@@ -419,9 +429,8 @@
     pl.semaphore_wait(barrier, len(everyone))
 
     edge = pl.ds(length, EDGE)
-    links.start(
-        residual_ref.at[pl.ds(length - EDGE, EDGE), :], w.normed.at[edge, :], w.tail_s, w.tail_r, peers[0]
-    )
+    loads[0].wait()
+    links.start(w.edge, w.normed.at[edge, :], w.tail_s, w.tail_r, peers[0])
     share = depth // CHUNKS
 
     def gather(n):
@@ -457,6 +466,8 @@
         columns = pl.ds(j * PIECE, PIECE)
         links.arrived(w.gate.at[pl.ds(ahead, 2 * depth), columns], w.forward_r.at[j])
 
+    gather(0)
+    gather(1)
     for load in loads[3:]:
         load.start()
 
@@ -467,20 +478,27 @@
         w.normed[place, :] = (wide * factor * mix_gain_ref[...]).astype(jnp.bfloat16)
 
     def norm_step(i, carry):
-        norm(aligned(i, unit), unit)
+        norm(aligned(i, 8), 8)
         return carry
 
-    for load in small_loads:
+    def to_inner(rows):
+        w.inner[rows, :] = jnp.dot(
+            w.normed[rows, :], w.in_proj[...], preferred_element_type=jnp.float32
+        ).astype(jnp.bfloat16)
+
+    small_loads[0].wait()
+    for k in range(PARTS):
+        row_loads[k].wait()
+        steps = part_rows // 8
+        lax.fori_loop(k * steps, (k + 1) * steps, norm_step, 0, unroll=4)
+    loads[1].wait()
+    to_inner(pl.ds(0, length))
+    links.arrived(w.normed.at[edge, :], w.tail_r)
+    gather(2)
+    norm(length, EDGE)
+    to_inner(edge)
+    for load in small_loads[1:]:
         load.wait()
-    loads[0].wait()
-    lax.fori_loop(0, 16, norm_step, 0, unroll=4)
-    links.arrived(w.normed.at[edge, :], w.tail_r)
-    gather(0)
-    norm(length, EDGE)
-    loads[1].wait()
-    w.inner[...] = jnp.dot(w.normed[...], w.in_proj[...], preferred_element_type=jnp.float32).astype(
-        jnp.bfloat16
-    )
     local_states(
         taps,
         links.s,
@@ -498,7 +516,7 @@
     )
     for k in range(count - 1):
         links.start(w.ends, w.arrived.at[k], w.end_s, w.end_r, peers[k])
-    for n in range(1, 2 * CHUNKS):
+    for n in range(3, 2 * CHUNKS):
         gather(n)
     loads[2].wait()
     branch = jax.nn.gelu(
@@ -626,8 +644,8 @@
             ).astype(jnp.bfloat16)
 
     give(0)
+    tokens.relay(0, 1)
     give(1)
-    tokens.relay(0, 1)
     for j in range(pieces):
         pass_on(j)
         if j + 2 < pieces:
@@ -635,8 +653,11 @@
         if j == 0:
             for i in range(2):
                 tokens.relayed(0, i)
+        if j == 1:
             links.arrived(hidden_in.at[links.xh, others, :], spread.pair_r.at[0])
-        keep(j)
+            keep(0)
+        if j > 0:
+            keep(j)
         if j > 1:
             take(j - 2)
 
@@ -767,6 +788,8 @@
         end_s=dma,
         end_r=dma,
         load=dma((8,)),
+        row_load=dma((PARTS,)),
+        edge=pltpu.VMEM((EDGE, width), bf),
         gather_s=dma,
         gather_r=dma((2, 2)),
         forward_s=dma,

time: 108 us -> 104 us (0.963)
  Pallas kernels: 106 us -> 103 us
    pallas_call x1, Pallas kernels: 106 us -> 103 us  [on_device(): pl.pallas_call(functools.partial(layer_kernel, count, conv_weight.shape[0...]
where the time goes in v6:
time: 104 us
  Pallas kernels  103 us (99%)
  local copies, waits for them, and re-layouts  1.32 us (1%)
    pallas_call x1, Pallas kernels, on_device(): pl.pallas_call(functools.partial(layer_kernel, count, conv_weight.shape[0...  103 us

profile of v6, /device:TPU:1, one launch (start us, length us, event | category | flops | bytes accessed | tf_op | source)
XLA Modules:
  0.0 104.0 jit_solution(17589636605062848065)
XLA Ops:
  0.0 102.7 %shard_map.154 = bf16[256,4096]{1,0:T(8,128)(2,1)S(1)} custom-call(f32[1,4096]{1,0:T(1,128)} %bitcast.6, f32[4,256]{1,0:T(4,128)} %refs_1_.1, f32[1,256]{1,0:T(1,128)} %bitcast.8, bf16[1,256,256]{2,1,0:T(8,128)(2,1)} %refs_3_.1, f32[1,256]{1,0:T(1,128)} %bitcast.9, bf16[1,256,256]{2,1,0:T(8,128)(2,1)} %refs_5_.1, f32[1,256]{1,0:T(1,128)} %bitcast.10, ...), custom_call_target="tpu_custom_call" | custom-call | tf_op jit(solution)/shard_map/pallas_call | solution.py:804
  102.7 1.3 %copy.18 = bf16[256,4096]{1,0:T(8,128)(2,1)} copy(bf16[256,4096]{1,0:T(8,128)(2,1)S(1)} %shard_map.154) | data formatting | bytes 4194304
